TPU v7x, 16 devices: a whole 2x2x2 slice. The times are simulated.
16 devices in a mesh: dp: 4 (over z, y), tp: 4 (over x, core).
Axes of the slice: x: 2, y: 2, z: 2, core: 2. Of those that a mesh axis runs over, the one named last changes fastest.
Arguments:
- resid_in: bfloat16 [1024, 2048], P('dp'), parts along dimension 0
- positions: int32 [1024], P('dp'), parts along dimension 0
- k_cache: bfloat16 [1024, 256, 8, 64], P('dp', None, 'tp'), parts along dimension 0
- v_cache: bfloat16 [1024, 256, 8, 64], P('dp', None, 'tp'), parts along dimension 0
- gain_attn: bfloat16 [2048], replicated
- w_query: bfloat16 [2048, 2048], P(None, 'tp')
- w_key: bfloat16 [2048, 512], P(None, 'tp')
- w_value: bfloat16 [2048, 512], P(None, 'tp')
- w_out: bfloat16 [2048, 2048], P('tp')
- gain_mlp: bfloat16 [2048], replicated
- w_gate: bfloat16 [2048, 8192], P(None, 'tp')
- w_up: bfloat16 [2048, 8192], P(None, 'tp')
- w_down: bfloat16 [8192, 2048], P('tp')
Outputs:
- output 1: bfloat16 [1024, 2048], P('dp'), parts along dimension 0
- output 2: bfloat16 [1024, 256, 8, 64], P('dp', None, 'tp'), parts along dimension 0
- output 3: bfloat16 [1024, 256, 8, 64], P('dp', None, 'tp'), parts along dimension 0
There are 4 independent parts. A program takes and returns all parts, laid end to end along the dimension named above; an argument that names none is the same for every part.
All inputs are finite; a program needn't handle non-finite values.
Results may differ from a plain program's by a relative error of at most 0.0103436.
Values sent between devices are 32-bit elements.
A program may use at most 1 GiB of HBM per device.

v0:
```python
import math
import jax
import jax.numpy as jnp
from jax import lax
from jax.sharding import PartitionSpec as P

EPS = 1e-5
ROPE_THETA = 500000.0
ROPE_FACTOR = 8.0
LOW_FACTOR = 1.0
HIGH_FACTOR = 4.0
ORIG_CTX = 8192.0


def rms_norm(rows_in, gain):
    rows_f = rows_in.astype(jnp.float32)
    mean_sq = jnp.mean(rows_f * rows_f, axis=-1, keepdims=True)
    return (rows_f * lax.rsqrt(mean_sq + EPS) * gain.astype(jnp.float32)).astype(jnp.bfloat16)


def rope_tables(positions, head_dim):
    half_dim = head_dim // 2
    exponents = jnp.arange(half_dim, dtype=jnp.float32) * (2.0 / head_dim)
    inv_freq = 1.0 / jnp.power(ROPE_THETA, exponents)
    wavelen = (2.0 * math.pi) / inv_freq
    smooth = (ORIG_CTX / wavelen - LOW_FACTOR) / (HIGH_FACTOR - LOW_FACTOR)
    blended = (1.0 - smooth) * inv_freq / ROPE_FACTOR + smooth * inv_freq
    inv_freq = jnp.where(wavelen < ORIG_CTX / HIGH_FACTOR, inv_freq,
                         jnp.where(wavelen > ORIG_CTX / LOW_FACTOR, inv_freq / ROPE_FACTOR, blended))
    angles = positions.astype(jnp.float32)[:, None] * inv_freq[None, :]
    return jnp.cos(angles), jnp.sin(angles)


def apply_rope(vectors, cos_t, sin_t):
    half_dim = vectors.shape[-1] // 2
    lower_half = vectors[..., :half_dim]
    upper_half = vectors[..., half_dim:]
    cos_b = cos_t[:, None, :]
    sin_b = sin_t[:, None, :]
    return jnp.concatenate([lower_half * cos_b - upper_half * sin_b,
                            upper_half * cos_b + lower_half * sin_b], axis=-1)


def attention_block(resid_in, positions, k_cache, v_cache, gain_attn, w_query, w_key, w_value):
    n_seqs = resid_in.shape[0]
    cache_len = k_cache.shape[1]
    kv_heads = k_cache.shape[2]
    head_dim = k_cache.shape[3]
    group_size = w_query.shape[1] // (kv_heads * head_dim)
    normed = rms_norm(resid_in, gain_attn)
    queries = jnp.dot(normed, w_query, preferred_element_type=jnp.float32).astype(jnp.bfloat16)
    key_new = jnp.dot(normed, w_key, preferred_element_type=jnp.float32).astype(jnp.bfloat16)
    value_new = jnp.dot(normed, w_value, preferred_element_type=jnp.float32).astype(jnp.bfloat16)
    cos_t, sin_t = rope_tables(positions, head_dim)
    queries = apply_rope(queries.reshape(n_seqs, kv_heads * group_size, head_dim).astype(jnp.float32), cos_t, sin_t)
    queries = queries.astype(jnp.bfloat16).reshape(n_seqs, kv_heads, group_size, head_dim)
    key_new = apply_rope(key_new.reshape(n_seqs, kv_heads, head_dim).astype(jnp.float32), cos_t, sin_t)
    key_new = key_new.astype(jnp.bfloat16)
    value_new = value_new.reshape(n_seqs, kv_heads, head_dim)
    slot_iota = lax.broadcasted_iota(jnp.int32, (n_seqs, cache_len), 1)
    slot_hit = (slot_iota == positions[:, None])[:, :, None, None]
    k_full = jnp.where(slot_hit, key_new[:, None], k_cache)
    v_full = jnp.where(slot_hit, value_new[:, None], v_cache)
    scores = jnp.einsum('bkgd,bskd->bkgs', queries, k_full, preferred_element_type=jnp.float32)
    scores = scores * (1.0 / math.sqrt(head_dim))
    valid = (slot_iota <= positions[:, None])[:, None, None, :]
    scores = jnp.where(valid, scores, -jnp.inf)
    attn_prob = jax.nn.softmax(scores, axis=-1).astype(jnp.bfloat16)
    attn_out = jnp.einsum('bkgs,bskd->bkgd', attn_prob, v_full, preferred_element_type=jnp.float32)
    attn_out = attn_out.astype(jnp.bfloat16).reshape(n_seqs, kv_heads * group_size * head_dim)
    return attn_out, k_full, v_full


def gated_hidden(normed, w_gate, w_up):
    gate_proj = jnp.dot(normed, w_gate, preferred_element_type=jnp.float32).astype(jnp.bfloat16)
    up_proj = jnp.dot(normed, w_up, preferred_element_type=jnp.float32).astype(jnp.bfloat16)
    return (jax.nn.silu(gate_proj.astype(jnp.float32)) * up_proj.astype(jnp.float32)).astype(jnp.bfloat16)


def solution(mesh):
    def layer_local(resid_in, positions, k_cache, v_cache, gain_attn, w_query, w_key, w_value,
                    w_out, gain_mlp, w_gate, w_up, w_down):
        attn_out, k_full, v_full = attention_block(resid_in, positions, k_cache, v_cache,
                                                   gain_attn, w_query, w_key, w_value)
        y_part = jnp.dot(attn_out, w_out, preferred_element_type=jnp.float32)
        y_sum = lax.psum(y_part, 'tp')
        resid_mid = (resid_in.astype(jnp.float32) + y_sum).astype(jnp.bfloat16)
        hidden = gated_hidden(rms_norm(resid_mid, gain_mlp), w_gate, w_up)
        z_part = jnp.dot(hidden, w_down, preferred_element_type=jnp.float32)
        z_sum = lax.psum(z_part, 'tp')
        resid_out = (resid_mid.astype(jnp.float32) + z_sum).astype(jnp.bfloat16)
        return resid_out, k_full, v_full

    row_spec = P('dp', None)
    cache_spec = P('dp', None, 'tp', None)
    col_spec = P(None, 'tp')
    split_rows = P('tp', None)
    return jax.shard_map(layer_local, mesh=mesh,
                         in_specs=(row_spec, P('dp'), cache_spec, cache_spec, P(), col_spec, col_spec,
                                   col_spec, split_rows, P(), col_spec, col_spec, split_rows),
                         out_specs=(row_spec, cache_spec, cache_spec), check_vma=False)
```

profile of v0, /device:TPU:0, one launch (start us, length us, event | category | flops | bytes accessed | tf_op | source)
XLA Modules:
  0.0 201.2 jit_solution(17181364524752197783)
XLA Ops:
  7.2 0.8 convert_element_type.84
  8.1 1.5 iota_compare_fusion.1
  9.5 1.6 fusion.7
  11.1 0.7 convert_element_type.79
  11.8 1.9 convolution_convert_fusion.5
  14.0 0.6 copy-done.4
  14.8 1.6 convolution_convert_fusion.4
  16.5 3.1 %fusion.15 = f32[256,512]{1,0:T(8,128)} fusion(bf16[2048,512]{1,0:T(8,128)(2,1)} %param.18, bf16[256,2048]{1,0:T(8,128)(2,1)S(1)} %copy-done.1, f32[2048]{0:T(1024)S(1)} %convert_element_type.79, f32[256]{0:T(256)S(1)} %add_rsqrt_fusion.1), kind=kOutput, calls=%fused_computation.32 | convolution fusion | flops 539230208 | bytes 3679232 | tf_op jit(solution)/shard_map/dot_general | solution.py:51
  19.7 2.0 %copy.20 = f32[256,512]{0,1:T(8,128)} copy(f32[256,512]{1,0:T(8,128)} %fusion.15) | data formatting | bytes 1048576 | tf_op jit(solution)/shard_map/convert_element_type | solution.py:55
  21.7 1.8 subtract_convert_fusion
  23.4 2.0 copy.21
  25.4 1.1 copy.22
  26.5 22.3 %broadcast_select_fusion.1 = (bf16[256,256,2,64]{1,3,2,0:T(8,128)(2,1)}, bf16[256,256,2,64]{1,3,2,0:T(8,128)(2,1)}) fusion(bf16[256,256,2,64]{1,3,2,0:T(8,128)(2,1)} %param.15, pred[256,256]{1,0:T(8,128)(4,1)} %get-tuple-element.14, bf16[256,2,64]{2,1,0:T(2,128)(2,1)S(1)} %copy.23, bf16[256,256,2,64]{1,3,2,0:T(8,128)(2,1)} %param.16, ...), kind=kLoop, calls=%fused_computation.2 | loop fusion | flops 16777216 | bytes 67305472 | tf_op jit(solution)/shard_map/jit(_where)/select_n | solution.py:62
  48.8 8.9 %fusion.29 = (f32[256,2,4]{2,1,0:T(2,128)S(1)}, f32[256,2,4,256]{3,2,1,0:T(4,128)}) fusion(bf16[256,256,2,64]{1,3,2,0:T(8,128)(2,1)} %get-tuple-element.9, pred[256,256]{1,0:T(8,128)(4,1)S(1)} %copy-done.6, bf16[256,2,4,32]{3,2,1,0:T(4,128)(2,1)} %bitcast.18, bf16[256,2,4,32]{3,2,1,0:T(4,128)(2,1)} %bitcast.17), kind=kOutput, calls=%fused_computation.54 | convolution fusion | flops 69730560 | bytes 19210240 | tf_op jit(solution)/shard_map/sub | solution.py:68
  57.8 9.5 %convolution_convert_fusion.2 = bf16[256,2,4,64]{3,2,1,0:T(4,128)(2,1)} fusion(bf16[256,256,2,64]{1,3,2,0:T(8,128)(2,1)} %get-tuple-element.10, f32[256,2,4,256]{3,2,1,0:T(4,128)} %get-tuple-element.16, f32[256,2,4]{2,1,0:T(2,128)S(1)} %get-tuple-element.15), kind=kOutput, calls=%fused_computation.30 | convolution fusion | flops 68288512 | bytes 19144704 | tf_op jit(solution)/shard_map/bkgs,bskd->bkgd/dot_general | solution.py:69
  67.2 1.3 copy.25
  68.6 2.0 %fusion.32 = f32[256,2048]{1,0:T(8,128)} fusion(bf16[256,512]{0,1:T(8,128)(2,1)S(1)} %bitcast.20, bf16[512,2048]{1,0:T(8,128)(2,1)S(1)} %copy-done), kind=kOutput, calls=%fused_computation.55 | convolution fusion | flops 536870912 | bytes 4456448 | tf_op jit(solution)/shard_map/dot_general | solution.py:85
  71.3 49.8 %all-reduce.3.cloned.1.call-done = f32[256,2048]{1,0:T(8,128)} async-done(((f32[256,2048]{1,0:T(8,128)}), f32[256,2048]{1,0:T(8,128)}) %all-reduce.3.cloned.1.call-update) | async-done | bytes 2097168 | tf_op jit(solution)/shard_map/psum | solution.py:86
  121.1 2.0 fusion.11
  123.1 1.0 copy-done.2
  124.0 7.2 %convert_multiply_fusion.4 = f32[256,2048]{1,0:T(8,128)} fusion(bf16[2048,2048]{1,0:T(8,128)(2,1)} %param.23, bf16[256,2048]{1,0:T(8,128)(2,1)S(1)} %get-tuple-element.4, f32[2048]{0:T(1024)S(1)} %convert_element_type.93, f32[256]{0:T(256)S(1)} %add_rsqrt_fusion), kind=kOutput, calls=%fused_computation.9 | convolution fusion | flops 2152726528 | bytes 11543552 | tf_op jit(solution)/shard_map/dot_general | solution.py:75
  131.2 12.6 %fusion.17 = f32[256,2048]{1,0:T(8,128)} fusion(bf16[2048,2048]{1,0:T(8,128)(2,1)} %param.25, f32[256,2048]{1,0:T(8,128)} %convert_multiply_fusion.4, bf16[2048,2048]{1,0:T(8,128)(2,1)} %param.24, bf16[256,2048]{1,0:T(8,128)(2,1)} %copy-done.2, f32[2048]{0:T(1024)S(1)} %convert_element_type.93, f32[256]{0:T(256)S(1)} %add_rsqrt_fusion), kind=kOutput, calls=%fused_computation.36 | convolution fusion | flops 4299161600 | bytes 22029312 | tf_op jit(solution)/shard_map/dot_general | solution.py:89
  143.8 47.7 %all-reduce.5.cloned.1.call-done = f32[256,2048]{1,0:T(8,128)} async-done(((f32[256,2048]{1,0:T(8,128)}), f32[256,2048]{1,0:T(8,128)}) %all-reduce.5.cloned.1.call-update) | async-done | bytes 2097168 | tf_op jit(solution)/shard_map/psum | solution.py:90
  191.5 2.8 %fusion.14 = bf16[256,2048]{1,0:T(8,128)(2,1)} fusion(f32[256,2048]{1,0:T(8,128)} %all-reduce.5.cloned.1.call-done, bf16[256,2048]{1,0:T(8,128)(2,1)S(1)} %copy-done.3), kind=kLoop, calls=%fused_computation.26 | loop fusion | flops 1572864 | bytes 4194304 | tf_op jit(solution)/shard_map/convert_element_type | solution.py:91
  (28 shorter events, 1.3 us)
Async XLA Ops:
  7.2 61.4 %copy-start = (bf16[512,2048]{1,0:T(8,128)(2,1)S(1)}, bf16[512,2048]{1,0:T(8,128)(2,1)}, u32[]{:S(2)}) copy-start(bf16[512,2048]{1,0:T(8,128)(2,1)} %param.21) | copy-start | bytes 6291460
  7.2 113.9 %all-reduce.3.cloned.1.call-start = ((), (), s32[]{:S(2)}) async-start(), calls=%async_computation | async-start | bytes 4194304 | tf_op jit(solution)/shard_map/psum | solution.py:86
  9.5 5.2 %copy-start.1 = (bf16[256,2048]{1,0:T(8,128)(2,1)S(1)}, bf16[256,2048]{1,0:T(8,128)(2,1)}, u32[]{:S(2)}) copy-start(bf16[256,2048]{1,0:T(8,128)(2,1)} %param.13) | copy-start | bytes 3145732
  14.0 0.6 copy-start.4
  14.0 0.6 copy-start.5
  26.5 22.3 %copy-start.6 = (pred[256,256]{1,0:T(8,128)(4,1)S(1)}, pred[256,256]{1,0:T(8,128)(4,1)}, u32[]{:S(2)}) copy-start(pred[256,256]{1,0:T(8,128)(4,1)} %get-tuple-element.13) | copy-start | bytes 196612
  70.6 0.7 copy-start.7
  70.6 120.9 %all-reduce.5.cloned.1.call-start = ((), (), s32[]{:S(2)}) async-start(), calls=%async_computation.1 | async-start | bytes 4194304 | tf_op jit(solution)/shard_map/psum | solution.py:90
  123.1 1.0 copy-start.2
  143.8 47.7 %copy-start.3 = (bf16[256,2048]{1,0:T(8,128)(2,1)S(1)}, bf16[256,2048]{1,0:T(8,128)(2,1)}, u32[]{:S(2)}) copy-start(bf16[256,2048]{1,0:T(8,128)(2,1)} %copy-done.2) | copy-start | bytes 3145732
Sparse Core Ops, SparseCore 0:
  70.8 50.2 all-reduce.2
  143.9 47.5 all-reduce.4
where the time goes:
time: 202 us; the launch traced here: 201 us
  waiting for transfers between devices  97.5 us (48%)
  matrix products  46.9 us (23%)
  other arithmetic  33.7 us (17%)
  between operations  14.2 us (7%)
  local copies, waits for them, and re-layouts  8.64 us (4%)
    psum x1, waiting for transfers between devices, layer_local(): y_sum = lax.psum(y_part, 'tp')  49.8 us
    psum x1, waiting for transfers between devices, layer_local(): z_sum = lax.psum(z_part, 'tp')  47.7 us
    select_n x1, other arithmetic, attention_block(): k_full = jnp.where(slot_hit, key_new[:, None], k_cache)  22.3 us
    dot_general x1, matrix products, layer_local(): z_part = jnp.dot(hidden, w_down, preferred_element_type=jnp.float32)  12.6 us
    dot_general x1, matrix products, attention_block(): jnp.einsum('bkgs,bskd->bkgd', attn_prob, v_full, preferred_element_type=j...  9.46 us
    sub x1, matrix products, attention_block(): attn_prob = jax.nn.softmax(scores, axis=-1).astype(jnp.bfloat16)  8.94 us
    dot_general x1, matrix products, gated_hidden(): jnp.dot(normed, w_gate, preferred_element_type=jnp.float32)  7.19 us
  transfers between devices with their start and end apart: 2, of which 2 were waited for; matrix products, arithmetic and copies ran while one was open for 0% of the time, Pallas kernels for 0%

commit v1 on v0

v1 whole, which is shorter than its diff:
```python
import functools
import math
import numpy as np
import jax
import jax.numpy as jnp
from jax import lax
from jax.experimental import pallas as pl
from jax.experimental.pallas import tpu as pltpu
from jax.sharding import PartitionSpec as P

EPS = 1e-5
ROPE_THETA = 500000.0
ROPE_FACTOR = 8.0
LOW_FACTOR = 1.0
HIGH_FACTOR = 4.0
ORIG_CTX = 8192.0
MESH = pl.DeviceIdType.MESH
F32 = jnp.float32
BF16 = jnp.bfloat16

HEAD = 64
PAIR = 128
GROUP = 4
SEQS = 16
SUB = 8


def frequency_lanes():
    half = HEAD // 2
    exponents = np.arange(half, dtype=np.float32) * np.float32(2.0 / HEAD)
    inv_freq = (1.0 / np.power(np.float32(ROPE_THETA), exponents)).astype(np.float32)
    wavelen = (2.0 * math.pi) / inv_freq
    smooth = (ORIG_CTX / wavelen - LOW_FACTOR) / (HIGH_FACTOR - LOW_FACTOR)
    blended = (1.0 - smooth) * inv_freq / ROPE_FACTOR + smooth * inv_freq
    inv_freq = np.where(wavelen < ORIG_CTX / HIGH_FACTOR, inv_freq,
                        np.where(wavelen > ORIG_CTX / LOW_FACTOR, inv_freq / ROPE_FACTOR, blended))
    lanes = np.arange(PAIR)
    freq = inv_freq[lanes % half].astype(np.float32)
    sign = np.where(lanes % HEAD < half, -1.0, 1.0).astype(np.float32)
    return np.stack([freq, sign])


def attention_kernel(pos_smem, pos_row, freq_ref, resid_ref, gain_ref, wq_ref, wk_ref, wv_ref, kc_ref, vc_ref,
                     o_ref, ko_ref, vo_ref, h_scr, q_scr, k_scr, v_scr, pos_scr):
    step = pl.program_id(0)
    n_seqs, dim = resid_ref.shape
    cache_len = kc_ref.shape[1]

    @pl.when(step == 0)
    def _project():
        rows = 64
        for i in range(n_seqs // rows):
            x = resid_ref[i * rows:(i + 1) * rows, :].astype(F32)
            mean_sq = jnp.sum(x * x, axis=1, keepdims=True) * (1.0 / dim)
            h_scr[i * rows:(i + 1) * rows, :] = (x * lax.rsqrt(mean_sq + EPS) * gain_ref[...].astype(F32)).astype(BF16)
        diag = (lax.broadcasted_iota(jnp.int32, (n_seqs, n_seqs), 0)
                == lax.broadcasted_iota(jnp.int32, (n_seqs, n_seqs), 1))
        pos_col = jnp.sum(jnp.where(diag, pos_row[...].astype(F32), 0.0), axis=1, keepdims=True)
        pos_scr[...] = jnp.broadcast_to(pos_col, (n_seqs, PAIR))
        angles = pos_scr[...] * freq_ref[0:1, :]
        cos_t = jnp.cos(angles)
        sin_t = jnp.sin(angles) * freq_ref[1:2, :]
        lane = lax.broadcasted_iota(jnp.int32, (n_seqs, PAIR), 1)
        low = lane % HEAD < HEAD // 2
        first = lane < HEAD

        def rope(t):
            t = t.astype(BF16).astype(F32)
            swapped = jnp.where(low, pltpu.roll(t, PAIR - HEAD // 2, 1), pltpu.roll(t, HEAD // 2, 1))
            return (t * cos_t + swapped * sin_t).astype(BF16).astype(F32)

        h = h_scr[...]
        tiles = [rope(jnp.dot(h, wq_ref[:, t * PAIR:(t + 1) * PAIR], preferred_element_type=F32)) for t in range(GROUP)]
        for g in range(GROUP):
            lower, upper = tiles[g // 2], tiles[2 + g // 2]
            if g % 2 == 0:
                upper = pltpu.roll(upper, HEAD, 1)
            else:
                lower = pltpu.roll(lower, HEAD, 1)
            q_scr[g, :, :] = jnp.where(first, lower, upper)
        k_scr[...] = rope(jnp.dot(h, wk_ref[...], preferred_element_type=F32))
        v_scr[...] = jnp.dot(h, wv_ref[...], preferred_element_type=F32).astype(BF16).astype(F32)

    lane_s = lax.broadcasted_iota(jnp.int32, (PAIR, cache_len), 1)
    lane_q = lax.broadcasted_iota(jnp.int32, (SUB, PAIR), 1)
    sub_q = lax.broadcasted_iota(jnp.int32, (SUB, PAIR), 0)
    head_mask = [lane_q < HEAD, lane_q >= HEAD]
    lane_p = lax.broadcasted_iota(jnp.int32, (SUB, cache_len), 1)
    o_parts = [[] for _ in range(GROUP)]
    for t in range(SEQS // SUB):
        base = pl.multiple_of(step * SEQS + t * SUB, SUB)
        k_t = k_scr[pl.ds(base, SUB), :].T
        v_t = v_scr[pl.ds(base, SUB), :].T
        for b in range(SUB):
            hit = lane_s == pos_smem[base + b]
            lo = (t * SUB + b) * PAIR
            ko_ref[lo:lo + PAIR, :] = jnp.where(hit, k_t[:, b:b + 1], kc_ref[lo:lo + PAIR, :].astype(F32)).astype(BF16)
            vo_ref[lo:lo + PAIR, :] = jnp.where(hit, v_t[:, b:b + 1], vc_ref[lo:lo + PAIR, :].astype(F32)).astype(BF16)
        lo = t * SUB * PAIR
        k_blk = ko_ref[lo:lo + SUB * PAIR, :]
        v_blk = vo_ref[lo:lo + SUB * PAIR, :]
        q_rows = []
        for g in range(GROUP):
            q_g = q_scr[g, pl.ds(base, SUB), :]
            for h in range(2):
                q_h = jnp.where(head_mask[h], q_g, 0.0)
                q_rows.append(jnp.concatenate([jnp.where(sub_q == b, q_h, 0.0) for b in range(SUB)], axis=1))
        q_bd = jnp.concatenate(q_rows, axis=0).astype(BF16)
        scores = jnp.dot(q_bd, k_blk, preferred_element_type=F32) * (1.0 / math.sqrt(HEAD))
        pos8 = pos_scr[pl.ds(base, SUB), 0:1].astype(jnp.int32)
        valid = lane_p <= pos8
        scores = jnp.where(jnp.concatenate([valid] * (2 * GROUP), axis=0), scores, -jnp.inf)
        top = jnp.max(scores, axis=1, keepdims=True)
        expd = jnp.exp(scores - top)
        prob = (expd / jnp.sum(expd, axis=1, keepdims=True)).astype(BF16)
        mixed = lax.dot_general(prob, v_blk, (((1,), (1,)), ((), ())), preferred_element_type=F32)
        for g in range(GROUP):
            acc = None
            for h in range(2):
                r = (g * 2 + h) * SUB
                part = mixed[r:r + SUB, 0:PAIR]
                for b in range(1, SUB):
                    part = jnp.where(sub_q == b, mixed[r:r + SUB, b * PAIR:(b + 1) * PAIR], part)
                acc = part if acc is None else jnp.where(head_mask[1], part, acc)
            o_parts[g].append(acc)
    for g in range(GROUP):
        o_ref[:, g * PAIR:(g + 1) * PAIR] = jnp.concatenate(o_parts[g], axis=0).astype(BF16)


def attention_call(resid_in, positions, kc, vc, gain, w_query, w_key, w_value):
    n_seqs, dim = resid_in.shape
    cache_len = kc.shape[1]
    rows = SEQS * PAIR
    whole = lambda shape: pl.BlockSpec(shape, lambda i, p: (0,) * len(shape))
    cache_spec = pl.BlockSpec((rows, cache_len), lambda i, p: (i, 0))
    freq = jnp.asarray(frequency_lanes())
    return pl.pallas_call(
        attention_kernel,
        out_shape=(jax.ShapeDtypeStruct((n_seqs, 2 * GROUP * HEAD), BF16),
                   jax.ShapeDtypeStruct(kc.shape, BF16), jax.ShapeDtypeStruct(vc.shape, BF16)),
        grid_spec=pltpu.PrefetchScalarGridSpec(
            num_scalar_prefetch=1, grid=(n_seqs // SEQS,),
            in_specs=[whole((1, n_seqs)), whole((2, PAIR)), whole((n_seqs, dim)), whole((1, dim)), whole(w_query.shape),
                      whole(w_key.shape), whole(w_value.shape), cache_spec, cache_spec],
            out_specs=(pl.BlockSpec((SEQS, 2 * GROUP * HEAD), lambda i, p: (i, 0)), cache_spec, cache_spec),
            scratch_shapes=[pltpu.VMEM((n_seqs, dim), BF16), pltpu.VMEM((GROUP, n_seqs, PAIR), F32),
                            pltpu.VMEM((n_seqs, PAIR), F32), pltpu.VMEM((n_seqs, PAIR), F32),
                            pltpu.VMEM((n_seqs, PAIR), F32)]),
        compiler_params=pltpu.CompilerParams(dimension_semantics=("arbitrary",), vmem_limit_bytes=48 << 20),
        name="attention",
    )(positions, positions.reshape(1, n_seqs), freq, resid_in, gain.reshape(1, dim), w_query, w_key, w_value, kc, vc)


N_CHUNK = 4
N_HALF = 2


def mlp_kernel(o_ref, resid_ref, gain_ref, wo_hbm, wg_hbm, wu_hbm, wd_hbm, out_ref,
               wo_v, wg_v, wu_v, wd_v, part, near, mine, far, full, h_scr, a_scr,
               wo_sem, w_sem, near_send, near_recv, far_send, far_recv, back_send, back_recv):
    tp = lax.axis_index("tp")
    dp = lax.axis_index("dp")
    core = lax.rem(tp, 2)
    other = 1 - core
    sibling = tp + 1 - 2 * core
    partner = lax.rem(tp + 2, 4)
    n_seqs = o_ref.shape[0]
    half_dim = resid_ref.shape[1] // 2
    ffn = wg_v.shape[1]
    rows = n_seqs // N_CHUNK

    wo_copies = []
    for g in range(GROUP):
        for h in range(2):
            for s in range(2):
                wo_copies.append(pltpu.make_async_copy(
                    wo_hbm.at[pl.ds((h * GROUP + g) * HEAD, HEAD), pl.ds(s * half_dim, half_dim)],
                    wo_v.at[s, pl.ds((2 * g + h) * HEAD, HEAD), :], wo_sem.at[(2 * g + h) * 2 + s]))
    for c in wo_copies:
        c.start()
    w_copies = [pltpu.make_async_copy(src, dst, w_sem.at[i])
                for i, (src, dst) in enumerate(((wg_hbm, wg_v), (wu_hbm, wu_v), (wd_hbm, wd_v)))]
    for c in w_copies:
        c.start()

    barrier = pltpu.get_barrier_semaphore()
    for peer in (sibling, partner):
        pl.semaphore_signal(barrier, inc=1, device_id=(dp, peer), device_id_type=MESH)
    pl.semaphore_wait(barrier, 2)

    def remote(src, dst, sems, k, r, peer):
        return pltpu.make_async_remote_copy(src_ref=src, dst_ref=dst, send_sem=sems[0].at[k, r], recv_sem=sems[1].at[k, r],
                                            device_id=(dp, peer), device_id_type=MESH)

    def chunk(r):
        return pl.ds(r * rows, rows)

    def near_copy(k, r):
        return remote(part.at[k, other, chunk(r)], near.at[k, chunk(r)], (near_send, near_recv), k, r, sibling)

    def far_copy(k, r):
        return remote(mine.at[k, chunk(r)], far.at[k, chunk(r)], (far_send, far_recv), k, r, partner)

    def back_copy(k, r):
        return remote(full.at[k, core, chunk(r)], full.at[k, core, chunk(r)], (back_send, back_recv), k, r, sibling)

    def sum_near(k, r):
        near_copy(k, r).wait_recv()
        mine[k, chunk(r), :] = part[k, core, chunk(r), :] + near[k, chunk(r), :]
        far_copy(k, r).start()

    my_cols = pl.ds(pl.multiple_of(core * half_dim, half_dim), half_dim)
    other_cols = pl.ds(pl.multiple_of(other * half_dim, half_dim), half_dim)

    def sum_far_y(r):
        far_copy(0, r).wait_recv()
        total = resid_ref[chunk(r), my_cols].astype(F32) + (mine[0, chunk(r), :] + far[0, chunk(r), :])
        full[0, core, chunk(r), :] = total.astype(BF16).astype(F32)
        back_copy(0, r).start()

    def sum_far_z(r):
        far_copy(1, r).wait_recv()
        total = full[0, core, chunk(r), :] + (mine[1, chunk(r), :] + far[1, chunk(r), :])
        rounded = total.astype(BF16)
        full[1, core, chunk(r), :] = rounded.astype(F32)
        back_copy(1, r).start()
        out_ref[chunk(r), my_cols] = rounded

    for c in wo_copies:
        c.wait()
    for r in range(N_CHUNK):
        o = o_ref[chunk(r), :]
        part[0, other, chunk(r), :] = jnp.dot(o, wo_v[other], preferred_element_type=F32)
        near_copy(0, r).start()
        part[0, core, chunk(r), :] = jnp.dot(o, wo_v[core], preferred_element_type=F32)
        if r > 0:
            sum_near(0, r - 1)
    sum_near(0, N_CHUNK - 1)

    tile = 512
    per_half = N_CHUNK // N_HALF
    half_rows = n_seqs // N_HALF
    for m in range(N_HALF):
        for r in range(m * per_half, (m + 1) * per_half):
            sum_far_y(r)
        for r in range(m * per_half, (m + 1) * per_half):
            back_copy(0, r).wait_recv()
        for r in range(m * per_half, (m + 1) * per_half):
            x0 = full[0, 0, chunk(r), :]
            x1 = full[0, 1, chunk(r), :]
            mean_sq = (jnp.sum(x0 * x0, axis=1, keepdims=True)
                       + jnp.sum(x1 * x1, axis=1, keepdims=True)) * (0.5 / half_dim)
            inv = lax.rsqrt(mean_sq + EPS)
            at = pl.ds((r - m * per_half) * rows, rows)
            h_scr[at, :half_dim] = (x0 * inv * gain_ref[:, :half_dim].astype(F32)).astype(BF16)
            h_scr[at, half_dim:] = (x1 * inv * gain_ref[:, half_dim:].astype(F32)).astype(BF16)
        if m == 0:
            w_copies[0].wait()
            w_copies[1].wait()

        def up_tile(n, carry):
            cols = pl.ds(pl.multiple_of(n * tile, tile), tile)
            gate = jnp.dot(h_scr[...], wg_v[:, cols], preferred_element_type=F32).astype(BF16).astype(F32)
            up = jnp.dot(h_scr[...], wu_v[:, cols], preferred_element_type=F32).astype(BF16).astype(F32)
            a_scr[:, cols] = (gate * jax.nn.sigmoid(gate) * up).astype(BF16)
            return carry

        lax.fori_loop(0, ffn // tile, up_tile, 0)
        if m == 0:
            w_copies[2].wait()
        half_at = pl.ds(m * half_rows, half_rows)
        for s in (other, core):
            def down_tile(n, carry, s=s):
                cols = pl.ds(pl.multiple_of(s * half_dim + n * tile, tile), tile)
                part[1, s, half_at, pl.ds(pl.multiple_of(n * tile, tile), tile)] = jnp.dot(
                    a_scr[...], wd_v[:, cols], preferred_element_type=F32)
                return carry

            lax.fori_loop(0, half_dim // tile, down_tile, 0)
            if s is other:
                for r in range(m * per_half, (m + 1) * per_half):
                    near_copy(1, r).start()
        for r in range(m * per_half, (m + 1) * per_half):
            sum_near(1, r)

    for r in range(N_CHUNK):
        sum_far_z(r)
        if r > 0:
            back_copy(1, r - 1).wait_recv()
            out_ref[chunk(r - 1), other_cols] = full[1, other, chunk(r - 1), :].astype(BF16)
    back_copy(1, N_CHUNK - 1).wait_recv()
    out_ref[chunk(N_CHUNK - 1), other_cols] = full[1, other, chunk(N_CHUNK - 1), :].astype(BF16)
    for k in range(2):
        for r in range(N_CHUNK):
            near_copy(k, r).wait_send()
            far_copy(k, r).wait_send()
            back_copy(k, r).wait_send()


def mlp_call(o, resid_in, gain, w_out, w_gate, w_up, w_down):
    n_seqs, dim = resid_in.shape
    half = dim // 2
    ffn = w_gate.shape[1]
    vmem = pl.BlockSpec(memory_space=pltpu.VMEM)
    hbm = pl.BlockSpec(memory_space=pl.ANY)
    sems = pltpu.SemaphoreType.DMA((2, N_CHUNK))
    return pl.pallas_call(
        mlp_kernel,
        out_shape=jax.ShapeDtypeStruct((n_seqs, dim), BF16),
        in_specs=[vmem, vmem, vmem, hbm, hbm, hbm, hbm],
        out_specs=vmem,
        scratch_shapes=[
            pltpu.VMEM((2, w_out.shape[0], half), BF16), pltpu.VMEM(w_gate.shape, BF16),
            pltpu.VMEM(w_up.shape, BF16), pltpu.VMEM(w_down.shape, BF16),
            pltpu.VMEM((2, 2, n_seqs, half), F32), pltpu.VMEM((2, n_seqs, half), F32),
            pltpu.VMEM((2, n_seqs, half), F32), pltpu.VMEM((2, n_seqs, half), F32),
            pltpu.VMEM((2, 2, n_seqs, half), F32),
            pltpu.VMEM((n_seqs // N_HALF, dim), BF16), pltpu.VMEM((n_seqs // N_HALF, ffn), BF16),
            pltpu.SemaphoreType.DMA((16,)), pltpu.SemaphoreType.DMA((3,)),
            sems, sems, sems, sems, sems, sems],
        compiler_params=pltpu.CompilerParams(collective_id=0, has_side_effects=True, vmem_limit_bytes=60 << 20),
        name="mlp",
    )(o, resid_in, gain.reshape(1, dim), w_out, w_gate, w_up, w_down)


def solution(mesh):
    def layer_local(resid_in, positions, k_cache, v_cache, gain_attn, w_query, w_key, w_value,
                    w_out, gain_mlp, w_gate, w_up, w_down):
        n_seqs, cache_len, heads, dim = k_cache.shape
        flat = lambda c: jnp.transpose(c, (0, 2, 3, 1)).reshape(n_seqs * heads * dim, cache_len)
        back = lambda c: jnp.transpose(c.reshape(n_seqs, heads, dim, cache_len), (0, 3, 1, 2))
        o, k_full, v_full = attention_call(resid_in, positions, flat(k_cache), flat(v_cache),
                                           gain_attn, w_query, w_key, w_value)
        resid_out = mlp_call(o, resid_in, gain_mlp, w_out, w_gate, w_up, w_down)
        return resid_out, back(k_full), back(v_full)

    row_spec = P('dp', None)
    cache_spec = P('dp', None, 'tp', None)
    col_spec = P(None, 'tp')
    split_rows = P('tp', None)
    return jax.shard_map(layer_local, mesh=mesh,
                         in_specs=(row_spec, P('dp'), cache_spec, cache_spec, P(), col_spec, col_spec,
                                   col_spec, split_rows, P(), col_spec, col_spec, split_rows),
                         out_specs=(row_spec, cache_spec, cache_spec), check_vma=False)
```

time: 202 us -> 106 us (0.52)
  waiting for transfers between devices: 97.5 us -> 0 us
  Pallas kernels: 0 us -> 93.4 us
  matrix products: 46.9 us -> 0 us
  other arithmetic: 33.7 us -> 0 us
  between operations: 14.2 us -> 0.65 us
  local copies, waits for them, and re-layouts: 8.64 us -> 11.2 us
    psum x2 -> x0, waiting for transfers between devices: 97.5 us -> none  [the longest x1 49.8 us: layer_local(): y_sum = lax.psum(y_part, 'tp')]
    pallas_call x0 -> x2, Pallas kernels: none -> 93.4 us  [the longest x1 61.3 us: mlp_call(): pl.pallas_call(mlp_kernel, out_shape=jax.ShapeDtypeStruct((n_seqs, dim),...]
    dot_general x7 -> x0, matrix products: 37.9 us -> none  [the longest x1 12.6 us: layer_local(): z_part = jnp.dot(hidden, w_down, preferred_element_type=jnp.float32)]
    select_n x2 -> x0, other arithmetic: 22.3 us -> none  [the longest x1 22.3 us: attention_block(): k_full = jnp.where(slot_hit, key_new[:, None], k_cache)]
    sub x1 -> x0, matrix products: 8.94 us -> none  [attention_block(): attn_prob = jax.nn.softmax(scores, axis=-1).astype(jnp.bfloat16)]
    unnamed x16 -> x15, local copies, waits for them, and re-layouts: 1.99 us -> 9.26 us
    convert_element_type x5 -> x0, other arithmetic: 4.37 us -> none  [the longest x1 2.85 us: layer_local(): resid_out = (resid_mid.astype(jnp.float32) + z_sum).astype(jnp.bfloat16)]
    reduce_sum x2 -> x0, other arithmetic: 3.58 us -> none  [rms_norm(): mean_sq = jnp.mean(rows_f * rows_f, axis=-1, keepdims=True)]
  transfers between devices with their start and end apart: 2 -> 0, of which waited for: 2 -> 0; matrix products, arithmetic and copies ran while one was open for 0% -> 0% of each run, Pallas kernels for 0% -> 0%
where the time goes in v1:
time: 106 us; the launch traced here: 105 us
  Pallas kernels  93.4 us (88%)
  local copies, waits for them, and re-layouts  11.2 us (11%)
    pallas_call x1, Pallas kernels, mlp_call(): pl.pallas_call(mlp_kernel, out_shape=jax.ShapeDtypeStruct((n_seqs, dim),...  61.3 us
    pallas_call x1, Pallas kernels, attention_call(): pl.pallas_call(attention_kernel, out_shape=(jax.ShapeDtypeStruct((n_seqs,...  32.1 us
    unnamed x15, local copies, waits for them, and re-layouts  9.26 us

profile of v1, /device:TPU:0, one launch (start us, length us, event | category | flops | bytes accessed | tf_op | source)
XLA Modules:
  0.0 105.3 jit_solution(13778189817952517553)
XLA Ops:
  0.6 0.7 reshape.28.gain_ref
  1.3 1.3 %reshape.31.gain_ref = bf16[1,2048]{1,0:T(2,128)(2,1)} reshape(bf16[2048]{0:T(1024)(128)(2,1)} %param.23) | data formatting | bytes 8192 | tf_op jit(solution)/shard_map/reshape | solution.py:323
  2.6 0.0 copy-start
  2.6 1.2 %copy-done = bf16[256,2048]{1,0:T(8,128)(2,1)S(1)} copy-done((bf16[256,2048]{1,0:T(8,128)(2,1)S(1)}, bf16[256,2048]{1,0:T(8,128)(2,1)}, u32[]{:S(2)}) %copy-start) | copy-done | bytes 1048600
  3.8 0.0 copy-start.1
  3.8 1.6 %copy-done.1 = bf16[2048,512]{1,0:T(8,128)(2,1)S(1)} copy-done((bf16[2048,512]{1,0:T(8,128)(2,1)S(1)}, bf16[2048,512]{1,0:T(8,128)(2,1)}, u32[]{:S(2)}) %copy-start.1) | copy-done | bytes 2097176
  5.4 0.0 copy-start.2
  5.4 1.0 copy-done.2
  6.5 0.0 copy-start.3
  6.5 1.0 copy-done.3
  7.5 0.0 copy-start.5
  7.5 0.7 copy-done.5
  8.2 0.0 copy-start.6
  8.2 0.7 copy-done.6
  8.9 32.1 %attention.1 = (bf16[256,512]{1,0:T(8,128)(2,1)S(1)}, bf16[32768,256]{1,0:T(8,128)(2,1)}, bf16[32768,256]{1,0:T(8,128)(2,1)}) custom-call(s32[256]{0:T(256)S(1)} %copy-done.5, s32[1,256]{1,0:T(1,128)S(1)} %bitcast.13, f32[2,128]{1,0:T(2,128)S(1)} %copy-done.6, bf16[256,2048]{1,0:T(8,128)(2,1)S(1)} %copy-done, bf16[1,2048]{1,0:T(2,128)(2,1)S(1)} %reshape.28.gain_ref, ...), custom_call_target="tpu_custom_call" | custom-call | tf_op jit(solution)/shard_map/attention/pallas_call | solution.py:137
  41.0 0.0 copy-start.4
  41.0 0.7 copy-done.4
  41.7 61.3 %mlp.1 = bf16[256,2048]{1,0:T(8,128)(2,1)} custom-call(bf16[256,512]{1,0:T(8,128)(2,1)} %copy-done.4, bf16[256,2048]{1,0:T(8,128)(2,1)} %resid_ref.3, bf16[1,2048]{1,0:T(2,128)(2,1)} %reshape.31.gain_ref, bf16[512,2048]{1,0:T(8,128)(2,1)} %wo_hbm.1, bf16[2048,2048]{1,0:T(8,128)(2,1)} %wg_hbm.1, bf16[2048,2048]{1,0:T(8,128)(2,1)} %wu_hbm.1, ...), custom_call_target="tpu_custom_call" | custom-call | tf_op jit(solution)/shard_map/mlp/pallas_call | solution.py:307
  103.0 2.3 %copy.18 = bf16[256,2048]{1,0:T(8,128)(2,1)} copy(bf16[256,2048]{1,0:T(8,128)(2,1)} %mlp.1) | data formatting | bytes 2097152
Async XLA Ops:
  2.6 1.2 %copy-start = (bf16[256,2048]{1,0:T(8,128)(2,1)S(1)}, bf16[256,2048]{1,0:T(8,128)(2,1)}, u32[]{:S(2)}) copy-start(bf16[256,2048]{1,0:T(8,128)(2,1)} %resid_ref.3) | copy-start | bytes 3145732
  3.8 1.6 %copy-start.1 = (bf16[2048,512]{1,0:T(8,128)(2,1)S(1)}, bf16[2048,512]{1,0:T(8,128)(2,1)}, u32[]{:S(2)}) copy-start(bf16[2048,512]{1,0:T(8,128)(2,1)} %wq_ref.1) | copy-start | bytes 6291460
  5.4 1.0 copy-start.2
  6.5 1.0 copy-start.3
  7.5 0.7 copy-start.5
  8.2 0.7 copy-start.6
  41.0 0.7 copy-start.4

commit v2 on v0

v2 whole, which is shorter than its diff:
```python
import functools
import math
import numpy as np
import jax
import jax.numpy as jnp
from jax import lax
from jax.experimental import pallas as pl
from jax.experimental.pallas import tpu as pltpu
from jax.sharding import PartitionSpec as P

EPS = 1e-5
ROPE_THETA = 500000.0
ROPE_FACTOR = 8.0
LOW_FACTOR = 1.0
HIGH_FACTOR = 4.0
ORIG_CTX = 8192.0
MESH = pl.DeviceIdType.MESH
F32 = jnp.float32
BF16 = jnp.bfloat16

HEAD = 64
PAIR = 128
GROUP = 4
SEQS = 16
SUB = 8
ROWS = 32
N_HALF = 2
W_PARTS = 2
SLOTS = 6
AHEAD = 3


def frequency_lanes():
    half = HEAD // 2
    exponents = np.arange(half, dtype=np.float32) * np.float32(2.0 / HEAD)
    inv_freq = (1.0 / np.power(np.float32(ROPE_THETA), exponents)).astype(np.float32)
    wavelen = (2.0 * math.pi) / inv_freq
    smooth = (ORIG_CTX / wavelen - LOW_FACTOR) / (HIGH_FACTOR - LOW_FACTOR)
    blended = (1.0 - smooth) * inv_freq / ROPE_FACTOR + smooth * inv_freq
    inv_freq = np.where(wavelen < ORIG_CTX / HIGH_FACTOR, inv_freq,
                        np.where(wavelen > ORIG_CTX / LOW_FACTOR, inv_freq / ROPE_FACTOR, blended))
    lanes = np.arange(PAIR)
    freq = inv_freq[lanes % half].astype(np.float32)
    sign = np.where(lanes % HEAD < half, -1.0, 1.0).astype(np.float32)
    return np.stack([freq, sign])


def layer_kernel(pos_hbm, freq_hbm, resid_hbm, gain_a_hbm, gain_m_hbm, wq_hbm, wk_hbm, wv_hbm, kc_hbm, vc_hbm,
                 wo_hbm, wg_hbm, wu_hbm, wd_hbm,
                 x1_hbm, send_hbm, knew_hbm, vnew_hbm,
                 pos_v, freq_v, resid_v, gain_a, gain_m, wq_v, wk_v, wv_v, k_buf, v_buf, wo_v, wg_v, wu_v, wd_v,
                 h_scr, a_scr, q_scr, k_scr, v_scr, pos_scr, s_scr, p_scr, n_scr,
                 part, near, mine, far, full, zsum,
                 in_sem, kv_sem, wo_sem, w_sem, out_sem,
                 near_send, near_recv, far_send, far_recv, back_send, back_recv):
    tp = lax.axis_index("tp")
    dp = lax.axis_index("dp")
    core = lax.rem(tp, 2)
    other = 1 - core
    sibling = tp + 1 - 2 * core
    partner = lax.rem(tp + 2, 4)
    n_seqs, dim = resid_v.shape
    cache_len = kc_hbm.shape[1]
    half_dim = dim // 2
    ffn = wg_v.shape[1]
    n_chunk = n_seqs // ROWS
    block = ROWS * PAIR

    inputs = [pltpu.make_async_copy(src, dst, in_sem.at[i]) for i, (src, dst) in enumerate((
        (resid_hbm, resid_v), (gain_a_hbm, gain_a), (wq_hbm, wq_v), (wk_hbm, wk_v), (wv_hbm, wv_v),
        (pos_hbm, pos_v), (freq_hbm, freq_v), (gain_m_hbm, gain_m)))]
    for c in inputs:
        c.start()

    def cache_copies(r, slot):
        at = pl.ds(pl.multiple_of(r * block, block), block)
        return (pltpu.make_async_copy(kc_hbm.at[at], k_buf.at[slot], kv_sem.at[0, slot]),
                pltpu.make_async_copy(vc_hbm.at[at], v_buf.at[slot], kv_sem.at[1, slot]))

    for c in cache_copies(0, 0):
        c.start()
    wo_copies = []
    for g in range(GROUP):
        for h in range(2):
            for s in range(2):
                wo_copies.append(pltpu.make_async_copy(
                    wo_hbm.at[pl.ds((h * GROUP + g) * HEAD, HEAD), pl.ds(s * half_dim, half_dim)],
                    wo_v.at[s, pl.ds((2 * g + h) * HEAD, HEAD), :], wo_sem.at[(2 * g + h) * 2 + s]))
    for c in wo_copies:
        c.start()
    for c in cache_copies(1, 1):
        c.start()
    w_copies = []
    for src, dst in ((wg_hbm, wg_v), (wu_hbm, wu_v), (wd_hbm, wd_v)):
        rows = dst.shape[0] // W_PARTS
        for i in range(W_PARTS):
            at = pl.ds(i * rows, rows)
            w_copies.append(pltpu.make_async_copy(src.at[at], dst.at[at], w_sem.at[len(w_copies)]))

    barrier = pltpu.get_barrier_semaphore()
    for peer in (sibling, partner):
        pl.semaphore_signal(barrier, inc=1, device_id=(dp, peer), device_id_type=MESH)

    def remote(src, dst, sems, k, r, peer):
        return pltpu.make_async_remote_copy(src_ref=src, dst_ref=dst, send_sem=sems[0].at[k, r], recv_sem=sems[1].at[k, r],
                                            device_id=(dp, peer), device_id_type=MESH)

    def chunk(r):
        return pl.ds(pl.multiple_of(r * ROWS, ROWS), ROWS)

    def near_copy(k, r):
        return remote(part.at[other, chunk(r)], near.at[chunk(r)], (near_send, near_recv), k, r, sibling)

    def far_copy(r):
        return remote(mine.at[chunk(r)], far.at[chunk(r)], (far_send, far_recv), 0, r, partner)

    def back_copy(r):
        return remote(full.at[core, chunk(r)], full.at[core, chunk(r)], (back_send, back_recv), 0, r, sibling)

    def sum_near(r):
        near_copy(0, r).wait_recv()
        mine[chunk(r), :] = part[core, chunk(r), :] + near[chunk(r), :]
        far_copy(r).start()

    my_cols = pl.ds(pl.multiple_of(core * half_dim, half_dim), half_dim)
    other_cols = pl.ds(pl.multiple_of(other * half_dim, half_dim), half_dim)

    for c in inputs[:2]:
        c.wait()
    gain_row = gain_a[...].astype(F32).reshape(1, dim)
    rows = 64
    for i in range(n_seqs // rows):
        x = resid_v[i * rows:(i + 1) * rows, :].astype(F32)
        mean_sq = jnp.sum(x * x, axis=1, keepdims=True) * (1.0 / dim)
        h_scr[i * rows:(i + 1) * rows, :] = (x * lax.rsqrt(mean_sq + EPS) * gain_row).astype(BF16)
    for c in inputs[2:]:
        c.wait()
    diag = (lax.broadcasted_iota(jnp.int32, (n_seqs, n_seqs), 0)
            == lax.broadcasted_iota(jnp.int32, (n_seqs, n_seqs), 1))
    pos_col = jnp.sum(jnp.where(diag, pos_v[...].astype(F32), 0.0), axis=1, keepdims=True)
    pos_scr[...] = jnp.broadcast_to(pos_col, (n_seqs, PAIR))
    angles = pos_scr[...] * freq_v[0:1, :]
    cos_t = jnp.cos(angles)
    sin_t = jnp.sin(angles) * freq_v[1:2, :]
    lane = lax.broadcasted_iota(jnp.int32, (n_seqs, PAIR), 1)
    low = lane % HEAD < HEAD // 2
    first = lane < HEAD

    def rope(t):
        t = t.astype(BF16).astype(F32)
        swapped = jnp.where(low, pltpu.roll(t, PAIR - HEAD // 2, 1), pltpu.roll(t, HEAD // 2, 1))
        return (t * cos_t + swapped * sin_t).astype(BF16).astype(F32)

    h = h_scr[...]
    tiles = [rope(jnp.dot(h, wq_v[:, t * PAIR:(t + 1) * PAIR], preferred_element_type=F32)) for t in range(GROUP)]
    for g in range(GROUP):
        lower, upper = tiles[g // 2], tiles[2 + g // 2]
        if g % 2 == 0:
            upper = pltpu.roll(upper, HEAD, 1)
        else:
            lower = pltpu.roll(lower, HEAD, 1)
        q_scr[g, :, :] = jnp.where(first, lower, upper)
    k_scr[...] = rope(jnp.dot(h, wk_v[...], preferred_element_type=F32))
    v_scr[...] = jnp.dot(h, wv_v[...], preferred_element_type=F32).astype(BF16).astype(F32)
    new_copies = (pltpu.make_async_copy(k_scr, knew_hbm, out_sem.at[0]), pltpu.make_async_copy(v_scr, vnew_hbm, out_sem.at[1]))
    for c in new_copies:
        c.start()
    for c in wo_copies:
        c.wait()
    pl.semaphore_wait(barrier, 2)

    lane_q = lax.broadcasted_iota(jnp.int32, (SUB, PAIR), 1)
    sub_q = lax.broadcasted_iota(jnp.int32, (SUB, PAIR), 0)
    head_mask = [lane_q < HEAD, lane_q >= HEAD]
    lane_p = lax.broadcasted_iota(jnp.int32, (SUB, cache_len), 1).astype(F32)
    stack = lambda x: jnp.concatenate([x] * (2 * GROUP), axis=0)

    tall = 2 * GROUP * SUB

    def attend(r, slot):
        scale = 1.0 / math.sqrt(HEAD)
        tiles_at = [pl.multiple_of(r * ROWS + t * SUB, SUB) for t in range(ROWS // SUB)]
        for t, base in enumerate(tiles_at):
            q_rows = []
            for g in range(GROUP):
                q_g = q_scr[g, pl.ds(base, SUB), :]
                for hd in range(2):
                    q_rows.append(jnp.where(head_mask[hd], q_g, 0.0))
            q_bd = jnp.concatenate([jnp.concatenate([jnp.where(sub_q == b, q, 0.0) for b in range(SUB)], axis=1)
                                    for q in q_rows], axis=0).astype(BF16)
            q_all = jnp.concatenate(q_rows, axis=0)
            at = slice(t * tall, (t + 1) * tall)
            n_scr[at, :] = jnp.broadcast_to(
                jnp.sum(q_all * stack(k_scr[pl.ds(base, SUB), :]), axis=1, keepdims=True) * scale, (tall, PAIR))
            s_scr[at, :] = jnp.dot(q_bd, k_buf[slot, t * SUB * PAIR:(t + 1) * SUB * PAIR, :],
                                   preferred_element_type=F32) * scale
        for t, base in enumerate(tiles_at):
            at = slice(t * tall, (t + 1) * tall)
            old = stack(lane_p < pos_scr[pl.ds(base, SUB), 0:1])
            scores = jnp.where(old, s_scr[at, :], -jnp.inf)
            score_new = n_scr[at, 0:1]
            top = jnp.maximum(jnp.max(scores, axis=1, keepdims=True), score_new)
            expd = jnp.exp(scores - top)
            exp_new = jnp.exp(score_new - top)
            inv = 1.0 / (jnp.sum(expd, axis=1, keepdims=True) + exp_new)
            p_scr[at, :] = (expd * inv).astype(BF16)
            n_scr[at, :] = jnp.broadcast_to((exp_new * inv).astype(BF16).astype(F32), (tall, PAIR))
        outs = []
        for t, base in enumerate(tiles_at):
            v_new = v_scr[pl.ds(base, SUB), :]
            mixed = lax.dot_general(p_scr[t * tall:(t + 1) * tall, :], v_buf[slot, t * SUB * PAIR:(t + 1) * SUB * PAIR, :],
                                    (((1,), (1,)), ((), ())), preferred_element_type=F32)
            pieces = []
            for g in range(GROUP):
                acc = None
                for hd in range(2):
                    lo = (g * 2 + hd) * SUB
                    piece = mixed[lo:lo + SUB, 0:PAIR]
                    for b in range(1, SUB):
                        piece = jnp.where(sub_q == b, mixed[lo:lo + SUB, b * PAIR:(b + 1) * PAIR], piece)
                    piece = piece + n_scr[t * tall + lo:t * tall + lo + SUB, :] * v_new
                    acc = piece if acc is None else jnp.where(head_mask[1], piece, acc)
                pieces.append(acc)
            outs.append(jnp.concatenate(pieces, axis=1))
        return jnp.concatenate(outs, axis=0).astype(BF16)

    def chunk_step(r, carry):
        slot = lax.rem(r, 2)
        for c in cache_copies(r, slot):
            c.wait()
        o = attend(r, slot)

        @pl.when(r + 2 < n_chunk)
        def _next():
            for c in cache_copies(r + 2, slot):
                c.start()

        for i, c in enumerate(w_copies):
            pl.when(r == i + 1)(c.start)

        part[other, chunk(r), :] = jnp.dot(o, wo_v[other], preferred_element_type=F32)
        near_copy(0, r).start()
        part[core, chunk(r), :] = jnp.dot(o, wo_v[core], preferred_element_type=F32)

        @pl.when(r > 0)
        def _sum():
            sum_near(r - 1)
        return carry

    lax.fori_loop(0, n_chunk, chunk_step, 0)
    sum_near(n_chunk - 1)
    for r in range(n_chunk):
        near_copy(0, r).wait_send()

    def sum_far_y(r):
        far_copy(r).wait_recv()
        total = resid_v[chunk(r), my_cols].astype(F32) + (mine[chunk(r), :] + far[chunk(r), :])
        full[core, chunk(r), :] = total.astype(BF16).astype(F32)
        back_copy(r).start()

    sends = []
    gain_row2 = gain_m[...].astype(F32).reshape(1, dim)
    tile = 512
    per_half = n_chunk // N_HALF
    half_rows = n_seqs // N_HALF
    for m in range(N_HALF):
        chunks = range(m * per_half, (m + 1) * per_half)
        def normalize(r):
            back_copy(r).wait_recv()
            x0 = full[0, chunk(r), :]
            x1 = full[1, chunk(r), :]
            mean_sq = (jnp.sum(x0 * x0, axis=1, keepdims=True)
                       + jnp.sum(x1 * x1, axis=1, keepdims=True)) * (1.0 / dim)
            inv = lax.rsqrt(mean_sq + EPS)
            at = pl.ds((r - chunks[0]) * ROWS, ROWS)
            h_scr[at, :half_dim] = (x0 * inv * gain_row2[:, :half_dim]).astype(BF16)
            h_scr[at, half_dim:] = (x1 * inv * gain_row2[:, half_dim:]).astype(BF16)

        for r in chunks:
            sum_far_y(r)
            if r > chunks[0]:
                normalize(r - 1)
        normalize(chunks[-1])
        if m == 0:
            for c in w_copies[:2 * W_PARTS]:
                c.wait()

        def up_tile(n, carry):
            cols = pl.ds(pl.multiple_of(n * tile, tile), tile)
            h2 = h_scr[0:half_rows, :]
            gate = jnp.dot(h2, wg_v[:, cols], preferred_element_type=F32).astype(BF16).astype(F32)
            up = jnp.dot(h2, wu_v[:, cols], preferred_element_type=F32).astype(BF16).astype(F32)
            a_scr[:, cols] = (gate * jax.nn.sigmoid(gate) * up).astype(BF16)
            return carry

        lax.fori_loop(0, ffn // tile, up_tile, 0)
        if m == 0:
            for c in w_copies[2 * W_PARTS:]:
                c.wait()
        half_at = pl.ds(m * half_rows, half_rows)
        for s in (other, core):
            def down_tile(n, carry, s=s):
                cols = pl.ds(pl.multiple_of(s * half_dim + n * tile, tile), tile)
                part[s, half_at, pl.ds(pl.multiple_of(n * tile, tile), tile)] = jnp.dot(
                    a_scr[...], wd_v[:, cols], preferred_element_type=F32)
                return carry

            lax.fori_loop(0, half_dim // tile, down_tile, 0)
            if s is other:
                for r in chunks:
                    near_copy(1, r).start()
        for r in chunks:
            near_copy(1, r).wait_recv()
            zsum[chunk(r), :] = part[core, chunk(r), :] + near[chunk(r), :]
        sends += [pltpu.make_async_copy(full.at[core, half_at], x1_hbm.at[half_at], out_sem.at[4 + m]),
                  pltpu.make_async_copy(zsum.at[half_at], send_hbm.at[half_at], out_sem.at[2 + m])]
        for c in sends[-2:]:
            c.start()

    for c in (*new_copies, *sends):
        c.wait()
    for r in range(n_chunk):
        near_copy(1, r).wait_send()
        back_copy(r).wait_send()
        far_copy(r).wait_send()


def layer_call(resid_in, positions, kc, vc, gain_attn, w_query, w_key, w_value, w_out, gain_mlp, w_gate, w_up, w_down):
    n_seqs, dim = resid_in.shape
    half = dim // 2
    ffn = w_gate.shape[1]
    cache_len = kc.shape[1]
    n_chunk = n_seqs // ROWS
    hbm = pl.BlockSpec(memory_space=pl.ANY)
    sems = pltpu.SemaphoreType.DMA((2, n_chunk))
    freq = jnp.asarray(frequency_lanes())
    args = (positions.reshape(1, n_seqs), freq, resid_in, gain_attn, gain_mlp,
            w_query, w_key, w_value, kc, vc, w_out, w_gate, w_up, w_down)
    return pl.pallas_call(
        layer_kernel,
        out_shape=(jax.ShapeDtypeStruct((n_seqs, half), F32), jax.ShapeDtypeStruct((n_seqs, half), F32),
                   jax.ShapeDtypeStruct((n_seqs, PAIR), F32), jax.ShapeDtypeStruct((n_seqs, PAIR), F32)),
        in_specs=[hbm] * len(args),
        out_specs=(hbm,) * 4,
        scratch_shapes=[
            pltpu.VMEM((1, n_seqs), jnp.int32), pltpu.VMEM(freq.shape, F32), pltpu.VMEM((n_seqs, dim), BF16),
            pltpu.VMEM((dim,), BF16), pltpu.VMEM((dim,), BF16),
            pltpu.VMEM(w_query.shape, BF16), pltpu.VMEM(w_key.shape, BF16), pltpu.VMEM(w_value.shape, BF16),
            pltpu.VMEM((2, ROWS * PAIR, cache_len), BF16), pltpu.VMEM((2, ROWS * PAIR, cache_len), BF16),
            pltpu.VMEM((2, w_out.shape[0], half), BF16), pltpu.VMEM(w_gate.shape, BF16),
            pltpu.VMEM(w_up.shape, BF16), pltpu.VMEM(w_down.shape, BF16),
            pltpu.VMEM((n_seqs, dim), BF16), pltpu.VMEM((n_seqs // N_HALF, ffn), BF16),
            pltpu.VMEM((GROUP, n_seqs, PAIR), F32), pltpu.VMEM((n_seqs, PAIR), F32),
            pltpu.VMEM((n_seqs, PAIR), F32), pltpu.VMEM((n_seqs, PAIR), F32),
            pltpu.VMEM((2 * GROUP * ROWS, cache_len), F32), pltpu.VMEM((2 * GROUP * ROWS, cache_len), BF16),
            pltpu.VMEM((2 * GROUP * ROWS, PAIR), F32),
            pltpu.VMEM((2, n_seqs, half), F32), pltpu.VMEM((n_seqs, half), F32),
            pltpu.VMEM((n_seqs, half), F32), pltpu.VMEM((n_seqs, half), F32),
            pltpu.VMEM((2, n_seqs, half), F32), pltpu.VMEM((n_seqs, half), F32),
            pltpu.SemaphoreType.DMA((8,)), pltpu.SemaphoreType.DMA((2, 2)), pltpu.SemaphoreType.DMA((16,)),
            pltpu.SemaphoreType.DMA((3 * W_PARTS,)), pltpu.SemaphoreType.DMA((6,)),
            sems, sems, sems, sems, sems, sems],
        compiler_params=pltpu.CompilerParams(collective_id=0, has_side_effects=True, vmem_limit_bytes=67043328),
        name="layer",
    )(*args)


def write_kernel(first_step, n_steps, pos_smem, knew_hbm, vnew_hbm, kc_hbm, vc_hbm, *refs):
    ko_hbm, vo_hbm, k_buf, v_buf, knew, vnew, new_sem, in_sem, out_sem = refs[-9:]
    cache_len = kc_hbm.shape[1]
    block = SEQS * PAIR
    width = PAIR
    lane = lax.broadcasted_iota(jnp.int32, (PAIR, width), 1)

    def copies(step):
        slot = lax.rem(step, SLOTS)
        at = pl.ds(pl.multiple_of((first_step + step) * block, block), block)
        return ((pltpu.make_async_copy(kc_hbm.at[at], k_buf.at[slot], in_sem.at[0, slot]),
                 pltpu.make_async_copy(vc_hbm.at[at], v_buf.at[slot], in_sem.at[1, slot])),
                (pltpu.make_async_copy(k_buf.at[slot], ko_hbm.at[at], out_sem.at[0, slot]),
                 pltpu.make_async_copy(v_buf.at[slot], vo_hbm.at[at], out_sem.at[1, slot])))

    for step in range(min(AHEAD, n_steps)):
        for c in copies(step)[0]:
            c.start()
    news = (pltpu.make_async_copy(knew_hbm, knew, new_sem.at[0]), pltpu.make_async_copy(vnew_hbm, vnew, new_sem.at[1]))
    for c in news:
        c.start()
    for c in news:
        c.wait()

    def body(step, carry):
        slot = lax.rem(step, SLOTS)
        ins, outs = copies(step)
        for c in ins:
            c.wait()

        @pl.when(step + AHEAD < n_steps)
        def _next():
            @pl.when(step + AHEAD >= SLOTS)
            def _free():
                for c in copies(step + AHEAD - SLOTS)[1]:
                    c.wait()
            for c in copies(step + AHEAD)[0]:
                c.start()

        for t in range(SEQS // SUB):
            base = pl.multiple_of((first_step + step) * SEQS + t * SUB, SUB)
            k_t = knew[pl.ds(base, SUB), :].T
            v_t = vnew[pl.ds(base, SUB), :].T
            for b in range(SUB):
                pos = pos_smem[base + b]
                lo = pl.multiple_of(pos // width * width, width)
                hit = lane == pos - lo
                at = pl.ds((t * SUB + b) * PAIR, PAIR)
                cols = pl.ds(lo, width)
                k_buf[slot, at, cols] = jnp.where(hit, k_t[:, b:b + 1], k_buf[slot, at, cols].astype(F32)).astype(BF16)
                v_buf[slot, at, cols] = jnp.where(hit, v_t[:, b:b + 1], v_buf[slot, at, cols].astype(F32)).astype(BF16)
        for c in outs:
            c.start()
        return carry

    lax.fori_loop(0, n_steps, body, 0)
    for step in range(max(0, n_steps - SLOTS), n_steps):
        for c in copies(step)[1]:
            c.wait()


def write_call(positions, knew, vnew, kc, vc, first_step, n_steps, prev=()):
    cache_len = kc.shape[1]
    hbm = pl.BlockSpec(memory_space=pl.ANY)
    buf = pltpu.VMEM((SLOTS, SEQS * PAIR, cache_len), BF16)
    return pl.pallas_call(
        functools.partial(write_kernel, first_step, n_steps),
        out_shape=(jax.ShapeDtypeStruct(kc.shape, BF16), jax.ShapeDtypeStruct(vc.shape, BF16)),
        in_specs=[pl.BlockSpec(memory_space=pltpu.SMEM)] + [hbm] * (4 + len(prev)),
        out_specs=(hbm, hbm),
        scratch_shapes=[buf, buf, pltpu.VMEM(knew.shape, F32), pltpu.VMEM(vnew.shape, F32), pltpu.SemaphoreType.DMA((2,)),
                        pltpu.SemaphoreType.DMA((2, SLOTS)), pltpu.SemaphoreType.DMA((2, SLOTS))],
        input_output_aliases={5 + i: i for i in range(len(prev))},
        compiler_params=pltpu.CompilerParams(vmem_limit_bytes=60 << 20),
        cost_estimate=pl.CostEstimate(flops=10 ** 10, bytes_accessed=4 * SEQS * PAIR * cache_len * 2 * n_steps,
                                      transcendentals=0),
        name="write",
    )(positions, knew, vnew, kc, vc, *prev)


def join_kernel(core_smem, mine_ref, other_ref, out_ref):
    half = mine_ref.shape[1]
    low = core_smem[0] == 0
    mine, other = mine_ref[...], other_ref[...]
    out_ref[:, :half] = jnp.where(low, mine, other).astype(BF16)
    out_ref[:, half:] = jnp.where(low, other, mine).astype(BF16)


def join_call(mine, other):
    n_seqs, half = mine.shape
    rows = 128
    one = pl.BlockSpec((rows, half), lambda i, c: (i, 0))
    return pl.pallas_call(
        join_kernel,
        out_shape=jax.ShapeDtypeStruct((n_seqs, 2 * half), BF16),
        grid_spec=pltpu.PrefetchScalarGridSpec(
            num_scalar_prefetch=1, grid=(n_seqs // rows,), in_specs=[one, one],
            out_specs=pl.BlockSpec((rows, 2 * half), lambda i, c: (i, 0))),
        compiler_params=pltpu.CompilerParams(dimension_semantics=("arbitrary",), vmem_limit_bytes=8 << 20),
        name="join",
    )((lax.axis_index('tp') % 2).reshape(1), mine, other)


FAR = [(0, 2), (1, 3), (2, 0), (3, 1)]
NEAR = [(0, 1), (1, 0), (2, 3), (3, 2)]


def solution(mesh):
    def layer_local(resid_in, positions, k_cache, v_cache, gain_attn, w_query, w_key, w_value,
                    w_out, gain_mlp, w_gate, w_up, w_down):
        n_seqs, cache_len, heads, dim = k_cache.shape
        flat = lambda c: jnp.transpose(c, (0, 2, 3, 1)).reshape(n_seqs * heads * dim, cache_len)
        back = lambda c: jnp.transpose(c.reshape(n_seqs, heads, dim, cache_len), (0, 3, 1, 2))
        kc, vc = flat(k_cache), flat(v_cache)
        x1, send, knew, vnew = layer_call(resid_in, positions, kc, vc, gain_attn, w_query, w_key, w_value,
                                                     w_out, gain_mlp, w_gate, w_up, w_down)
        far = lax.ppermute(send, 'tp', FAR)
        k_full, v_full = write_call(positions, knew, vnew, kc, vc, 0, n_seqs // SEQS)
        far, k_full, v_full = lax.optimization_barrier((far, k_full, v_full))
        total = x1 + (send + far)
        total_other = lax.ppermute(total, 'tp', NEAR)
        resid_out = join_call(total, total_other)
        return resid_out, back(k_full), back(v_full)

    row_spec = P('dp', None)
    cache_spec = P('dp', None, 'tp', None)
    col_spec = P(None, 'tp')
    split_rows = P('tp', None)
    return jax.shard_map(layer_local, mesh=mesh,
                         in_specs=(row_spec, P('dp'), cache_spec, cache_spec, P(), col_spec, col_spec,
                                   col_spec, split_rows, P(), col_spec, col_spec, split_rows),
                         out_specs=(row_spec, cache_spec, cache_spec), check_vma=False)
```

time: 202 us -> 79.8 us (0.40)
  waiting for transfers between devices: 97.5 us -> 2.56 us
  Pallas kernels: 0 us -> 72.3 us
  matrix products: 46.9 us -> 0 us
  other arithmetic: 33.7 us -> 1.49 us
  between operations: 14.2 us -> 0.67 us
  local copies, waits for them, and re-layouts: 8.64 us -> 0.97 us
    psum x2 -> x0, waiting for transfers between devices: 97.5 us -> none  [the longest x1 49.8 us: layer_local(): y_sum = lax.psum(y_part, 'tp')]
    pallas_call x0 -> x3, Pallas kernels: none -> 72.3 us  [the longest x1 46.3 us: layer_call(): pl.pallas_call(layer_kernel, out_shape=(jax.ShapeDtypeStruct((n_seqs, hal...]
    dot_general x7 -> x0, matrix products: 37.9 us -> none  [the longest x1 12.6 us: layer_local(): z_part = jnp.dot(hidden, w_down, preferred_element_type=jnp.float32)]
    select_n x2 -> x0, other arithmetic: 22.3 us -> none  [the longest x1 22.3 us: attention_block(): k_full = jnp.where(slot_hit, key_new[:, None], k_cache)]
    sub x1 -> x0, matrix products: 8.94 us -> none  [attention_block(): attn_prob = jax.nn.softmax(scores, axis=-1).astype(jnp.bfloat16)]
    convert_element_type x5 -> x0, other arithmetic: 4.37 us -> none  [the longest x1 2.85 us: layer_local(): resid_out = (resid_mid.astype(jnp.float32) + z_sum).astype(jnp.bfloat16)]
    reduce_sum x2 -> x0, other arithmetic: 3.58 us -> none  [rms_norm(): mean_sq = jnp.mean(rows_f * rows_f, axis=-1, keepdims=True)]
    convert_element_type x2 -> x0, local copies, waits for them, and re-layouts: 3.36 us -> none  [the longest x1 2.04 us: attention_block(): queries.reshape(n_seqs, kv_heads * group_size, head_dim).astype(jnp.float32)]
  transfers between devices with their start and end apart: 2 -> 2, of which waited for: 2 -> 1; matrix products, arithmetic and copies ran while one was open for 0% -> 0% of each run, Pallas kernels for 0% -> 31%
where the time goes in v2:
time: 79.8 us; the launch traced here: 79.6 us
  Pallas kernels  72.3 us (91%)
  waiting for transfers between devices  2.56 us (3%)
  starting transfers between devices  1.65 us (2%)
  other arithmetic  1.49 us (2%)
  local copies, waits for them, and re-layouts  0.97 us (1%)
    pallas_call x1, Pallas kernels, layer_call(): pl.pallas_call(layer_kernel, out_shape=(jax.ShapeDtypeStruct((n_seqs, hal...  46.3 us
    pallas_call x1, Pallas kernels, write_call(): pl.pallas_call(functools.partial(write_kernel, first_step, n_steps), out_...  25 us
    ppermute x1, waiting for transfers between devices, layer_local(): total_other = lax.ppermute(total, 'tp', NEAR)  2.55 us
  transfers between devices with their start and end apart: 2, of which 1 were waited for; matrix products, arithmetic and copies ran while one was open for 0% of the time, Pallas kernels for 31%

profile of v2, /device:TPU:0, one launch (start us, length us, event | category | flops | bytes accessed | tf_op | source)
XLA Modules:
  0.0 79.6 jit_solution(2775211028802613251)
XLA Ops:
  0.6 46.3 %layer.1 = (f32[256,1024]{1,0:T(8,128)}, f32[256,1024]{1,0:T(8,128)}, f32[256,128]{1,0:T(8,128)}, f32[256,128]{1,0:T(8,128)}) custom-call(s32[1,256]{1,0:T(1,128)} %bitcast.18, f32[2,128]{1,0:T(2,128)} %constant.19.clone.freq_hbm, bf16[256,2048]{1,0:T(8,128)(2,1)} %resid_hbm.1, bf16[2048]{0:T(1024)(128)(2,1)} %gain_a_hbm.1, bf16[2048]{0:T(1024)(128)(2,1)} %gain_m_hbm.1, ...), custom_call_target="tpu_custom_call" | custom-call | tf_op jit(solution)/shard_map/layer/pallas_call | solution.py:339
  46.9 1.5 %collective-permute-start = (f32[256,1024]{1,0:T(8,128)}, f32[256,1024]{1,0:T(8,128)S(1)}, u32[]{:S(2)}, u32[]{:S(2)}) collective-permute-start(f32[256,1024]{1,0:T(8,128)} %get-tuple-element.13), channel_id=1, source_target_pairs={{0,2},{1,3},{2,0},{3,1},{4,6},{5,7},{6,4},{7,5},{8,10},{9,11},{10,... | collective-permute-start | bytes 3145736 | tf_op jit(solution)/shard_map/ppermute | solution.py:484
  48.4 0.0 copy-start
  48.4 0.0 copy-start.1
  48.4 25.0 %write.1 = (bf16[32768,256]{1,0:T(8,128)(2,1)}, bf16[32768,256]{1,0:T(8,128)(2,1)}) custom-call(s32[256]{0:T(256)} %pos_smem.1, f32[256,128]{1,0:T(8,128)} %get-tuple-element.14.knew_hbm, f32[256,128]{1,0:T(8,128)} %get-tuple-element.15.vnew_hbm, bf16[32768,256]{1,0:T(8,128)(2,1)} %bitcast.15, bf16[32768,256]{1,0:T(8,128)(2,1)} %bitcast.17), custom_call_target="tpu_custom_call" | custom-call | flops 10000000000 | bytes 67108864 | tf_op jit(solution)/shard_map/write/pallas_call | solution.py:433
  73.4 0.0 collective-permute-done
  73.4 0.0 copy-start.2
  73.5 1.0 %copy-done.2 = f32[256,1024]{1,0:T(8,128)} copy-done((f32[256,1024]{1,0:T(8,128)}, f32[256,1024]{1,0:T(8,128)S(1)}, u32[]{:S(2)}) %copy-start.2) | copy-done | bytes 1048600
  74.4 0.0 copy-done
  74.4 0.0 copy-done.1
  74.4 1.5 %add_add_fusion.mine_ref = f32[256,1024]{1,0:T(8,128)S(1)} fusion(f32[256,1024]{1,0:T(8,128)S(1)} %copy-done, f32[256,1024]{1,0:T(8,128)S(1)} %copy-done.1, f32[256,1024]{1,0:T(8,128)} %copy-done.2), kind=kLoop, calls=%fused_computation | loop fusion | flops 524288 | bytes 4194304 | tf_op jit(solution)/shard_map/add | solution.py:487
  75.9 0.1 collective-permute-start.1
  76.1 2.6 %collective-permute-done.1.other_ref = f32[256,1024]{1,0:T(8,128)S(1)} collective-permute-done((f32[256,1024]{1,0:T(8,128)S(1)}, f32[256,1024]{1,0:T(8,128)S(1)}, u32[]{:S(2)}, u32[]{:S(2)}) %collective-permute-start.1) | collective-permute-done | bytes 1048608 | tf_op jit(solution)/shard_map/ppermute | solution.py:488
  78.6 1.0 %join.1 = bf16[256,2048]{1,0:T(8,128)(2,1)} custom-call(s32[1]{0:T(128)} %bitcast.core_smem, f32[256,1024]{1,0:T(8,128)S(1)} %add_add_fusion.mine_ref, f32[256,1024]{1,0:T(8,128)S(1)} %collective-permute-done.1.other_ref), custom_call_target="tpu_custom_call" | custom-call | tf_op jit(solution)/shard_map/join/pallas_call | solution.py:460
Async XLA Ops:
  46.9 26.5 %collective-permute-start = (f32[256,1024]{1,0:T(8,128)}, f32[256,1024]{1,0:T(8,128)S(1)}, u32[]{:S(2)}, u32[]{:S(2)}) collective-permute-start(f32[256,1024]{1,0:T(8,128)} %get-tuple-element.13), channel_id=1, source_target_pairs={{0,2},{1,3},{2,0},{3,1},{4,6},{5,7},{6,4},{7,5},{8,10},{9,11},{10,... | collective-permute-start | bytes 3145736 | tf_op jit(solution)/shard_map/ppermute | solution.py:484
  48.4 26.0 %copy-start = (f32[256,1024]{1,0:T(8,128)S(1)}, f32[256,1024]{1,0:T(8,128)}, u32[]{:S(2)}) copy-start(f32[256,1024]{1,0:T(8,128)} %get-tuple-element.12) | copy-start | bytes 3145732
  48.4 26.0 %copy-start.1 = (f32[256,1024]{1,0:T(8,128)S(1)}, f32[256,1024]{1,0:T(8,128)}, u32[]{:S(2)}) copy-start(f32[256,1024]{1,0:T(8,128)} %get-tuple-element.13) | copy-start | bytes 3145732
  73.4 1.0 %copy-start.2 = (f32[256,1024]{1,0:T(8,128)}, f32[256,1024]{1,0:T(8,128)S(1)}, u32[]{:S(2)}) copy-start(f32[256,1024]{1,0:T(8,128)S(1)} %collective-permute-done) | copy-start | bytes 3145732
  75.9 2.7 %collective-permute-start.1 = (f32[256,1024]{1,0:T(8,128)S(1)}, f32[256,1024]{1,0:T(8,128)S(1)}, u32[]{:S(2)}, u32[]{:S(2)}) collective-permute-start(f32[256,1024]{1,0:T(8,128)S(1)} %add_add_fusion.mine_ref), channel_id=1, source_target_pairs={{0,1},{1,0},{2,3},{3,2},{4,5},{5,4},{6,7},{7,6},{8,9},{9,8},{10,11... | collective-permute-start | bytes 3145736 | tf_op jit(solution)/shard_map/ppermute | solution.py:488

commit v3 on v2

--- a/solution.py
+++ b/solution.py
@@ -24,10 +24,13 @@
 SEQS = 16
 SUB = 8
 ROWS = 32
-N_HALF = 2
-W_PARTS = 2
-SLOTS = 6
-AHEAD = 3
+BLOCK = 32
+FIRST = 64
+PARTS = ((0, 4), (4, 8))
+LAYER_VMEM = 67043328
+W_PARTS = 4
+SLOTS = 16
+AHEAD = 16
 
 
 def frequency_lanes():
@@ -64,7 +67,7 @@
     half_dim = dim // 2
     ffn = wg_v.shape[1]
     n_chunk = n_seqs // ROWS
-    block = ROWS * PAIR
+    block = BLOCK * PAIR
 
     inputs = [pltpu.make_async_copy(src, dst, in_sem.at[i]) for i, (src, dst) in enumerate((
         (resid_hbm, resid_v), (gain_a_hbm, gain_a), (wq_hbm, wq_v), (wk_hbm, wk_v), (wv_hbm, wv_v),
@@ -77,8 +80,6 @@
         return (pltpu.make_async_copy(kc_hbm.at[at], k_buf.at[slot], kv_sem.at[0, slot]),
                 pltpu.make_async_copy(vc_hbm.at[at], v_buf.at[slot], kv_sem.at[1, slot]))
 
-    for c in cache_copies(0, 0):
-        c.start()
     wo_copies = []
     for g in range(GROUP):
         for h in range(2):
@@ -86,10 +87,6 @@
                 wo_copies.append(pltpu.make_async_copy(
                     wo_hbm.at[pl.ds((h * GROUP + g) * HEAD, HEAD), pl.ds(s * half_dim, half_dim)],
                     wo_v.at[s, pl.ds((2 * g + h) * HEAD, HEAD), :], wo_sem.at[(2 * g + h) * 2 + s]))
-    for c in wo_copies:
-        c.start()
-    for c in cache_copies(1, 1):
-        c.start()
     w_copies = []
     for src, dst in ((wg_hbm, wg_v), (wu_hbm, wu_v), (wd_hbm, wd_v)):
         rows = dst.shape[0] // W_PARTS
@@ -127,44 +124,54 @@
 
     for c in inputs[:2]:
         c.wait()
+    for c in cache_copies(0, 0):
+        c.start()
     gain_row = gain_a[...].astype(F32).reshape(1, dim)
-    rows = 64
-    for i in range(n_seqs // rows):
-        x = resid_v[i * rows:(i + 1) * rows, :].astype(F32)
-        mean_sq = jnp.sum(x * x, axis=1, keepdims=True) * (1.0 / dim)
-        h_scr[i * rows:(i + 1) * rows, :] = (x * lax.rsqrt(mean_sq + EPS) * gain_row).astype(BF16)
+
+    def normalize_in(lo, hi):
+        for i in range(lo, hi, FIRST):
+            x = resid_v[i:i + FIRST, :].astype(F32)
+            mean_sq = jnp.sum(x * x, axis=1, keepdims=True) * (1.0 / dim)
+            h_scr[i:i + FIRST, :] = (x * lax.rsqrt(mean_sq + EPS) * gain_row).astype(BF16)
+
+    def project(lo, hi):
+        n = hi - lo
+        at = slice(lo, hi)
+        angles = pos_scr[at, :] * freq_v[0:1, :]
+        cos_t = jnp.cos(angles)
+        sin_t = jnp.sin(angles) * freq_v[1:2, :]
+        lane = lax.broadcasted_iota(jnp.int32, (n, PAIR), 1)
+        low = lane % HEAD < HEAD // 2
+        first = lane < HEAD
+
+        def rope(t):
+            t = t.astype(BF16).astype(F32)
+            swapped = jnp.where(low, pltpu.roll(t, PAIR - HEAD // 2, 1), pltpu.roll(t, HEAD // 2, 1))
+            return (t * cos_t + swapped * sin_t).astype(BF16).astype(F32)
+
+        h = h_scr[at, :]
+        q_all = jnp.dot(h, wq_v[...], preferred_element_type=F32)
+        tiles = [rope(q_all[:, t * PAIR:(t + 1) * PAIR]) for t in range(GROUP)]
+        for g in range(GROUP):
+            lower, upper = tiles[g // 2], tiles[2 + g // 2]
+            if g % 2 == 0:
+                upper = pltpu.roll(upper, HEAD, 1)
+            else:
+                lower = pltpu.roll(lower, HEAD, 1)
+            q_scr[g, at, :] = jnp.where(first, lower, upper)
+        k_scr[at, :] = rope(jnp.dot(h, wk_v[...], preferred_element_type=F32))
+        v_scr[at, :] = jnp.dot(h, wv_v[...], preferred_element_type=F32).astype(BF16).astype(F32)
+
+    normalize_in(0, FIRST)
     for c in inputs[2:]:
         c.wait()
+    for c in (*wo_copies, *cache_copies(1, 1)):
+        c.start()
     diag = (lax.broadcasted_iota(jnp.int32, (n_seqs, n_seqs), 0)
             == lax.broadcasted_iota(jnp.int32, (n_seqs, n_seqs), 1))
     pos_col = jnp.sum(jnp.where(diag, pos_v[...].astype(F32), 0.0), axis=1, keepdims=True)
     pos_scr[...] = jnp.broadcast_to(pos_col, (n_seqs, PAIR))
-    angles = pos_scr[...] * freq_v[0:1, :]
-    cos_t = jnp.cos(angles)
-    sin_t = jnp.sin(angles) * freq_v[1:2, :]
-    lane = lax.broadcasted_iota(jnp.int32, (n_seqs, PAIR), 1)
-    low = lane % HEAD < HEAD // 2
-    first = lane < HEAD
-
-    def rope(t):
-        t = t.astype(BF16).astype(F32)
-        swapped = jnp.where(low, pltpu.roll(t, PAIR - HEAD // 2, 1), pltpu.roll(t, HEAD // 2, 1))
-        return (t * cos_t + swapped * sin_t).astype(BF16).astype(F32)
-
-    h = h_scr[...]
-    tiles = [rope(jnp.dot(h, wq_v[:, t * PAIR:(t + 1) * PAIR], preferred_element_type=F32)) for t in range(GROUP)]
-    for g in range(GROUP):
-        lower, upper = tiles[g // 2], tiles[2 + g // 2]
-        if g % 2 == 0:
-            upper = pltpu.roll(upper, HEAD, 1)
-        else:
-            lower = pltpu.roll(lower, HEAD, 1)
-        q_scr[g, :, :] = jnp.where(first, lower, upper)
-    k_scr[...] = rope(jnp.dot(h, wk_v[...], preferred_element_type=F32))
-    v_scr[...] = jnp.dot(h, wv_v[...], preferred_element_type=F32).astype(BF16).astype(F32)
-    new_copies = (pltpu.make_async_copy(k_scr, knew_hbm, out_sem.at[0]), pltpu.make_async_copy(v_scr, vnew_hbm, out_sem.at[1]))
-    for c in new_copies:
-        c.start()
+    project(0, FIRST)
     for c in wo_copies:
         c.wait()
     pl.semaphore_wait(barrier, 2)
@@ -177,9 +184,9 @@
 
     tall = 2 * GROUP * SUB
 
-    def attend(r, slot):
+    def attend(first_row, slot):
         scale = 1.0 / math.sqrt(HEAD)
-        tiles_at = [pl.multiple_of(r * ROWS + t * SUB, SUB) for t in range(ROWS // SUB)]
+        tiles_at = [pl.multiple_of(first_row + t * SUB, SUB) for t in range(BLOCK // SUB)]
         for t, base in enumerate(tiles_at):
             q_rows = []
             for g in range(GROUP):
@@ -224,30 +231,39 @@
             outs.append(jnp.concatenate(pieces, axis=1))
         return jnp.concatenate(outs, axis=0).astype(BF16)
 
-    def chunk_step(r, carry):
-        slot = lax.rem(r, 2)
-        for c in cache_copies(r, slot):
-            c.wait()
-        o = attend(r, slot)
-
-        @pl.when(r + 2 < n_chunk)
-        def _next():
-            for c in cache_copies(r + 2, slot):
-                c.start()
-
-        for i, c in enumerate(w_copies):
-            pl.when(r == i + 1)(c.start)
-
-        part[other, chunk(r), :] = jnp.dot(o, wo_v[other], preferred_element_type=F32)
-        near_copy(0, r).start()
-        part[core, chunk(r), :] = jnp.dot(o, wo_v[core], preferred_element_type=F32)
-
-        @pl.when(r > 0)
-        def _sum():
-            sum_near(r - 1)
+    def pair_step(p, carry):
+        for slot in range(2):
+            r = 2 * p + slot
+            for c in cache_copies(r, slot):
+                c.wait()
+            o = attend(r * ROWS, slot)
+
+            @pl.when(r + 2 < n_chunk)
+            def _next(r=r, slot=slot):
+                for c in cache_copies(r + 2, slot):
+                    c.start()
+
+            for i, c in enumerate(w_copies):
+                if (2 * i // 3) % 2 == slot:
+                    pl.when(r == 2 * i // 3)(c.start)
+
+            @pl.when(r > 1)
+            def _sum(r=r):
+                sum_near(r - 1)
+
+            part[other, chunk(r), :] = jnp.dot(o, wo_v[other], preferred_element_type=F32)
+            near_copy(0, r).start()
+            part[core, chunk(r), :] = jnp.dot(o, wo_v[core], preferred_element_type=F32)
+
+            if slot == 0:
+                @pl.when(r == 0)
+                def _others():
+                    normalize_in(FIRST, n_seqs)
+                    project(FIRST, n_seqs)
+                    sum_near(0)
         return carry
 
-    lax.fori_loop(0, n_chunk, chunk_step, 0)
+    lax.fori_loop(0, n_chunk // 2, pair_step, 0)
     sum_near(n_chunk - 1)
     for r in range(n_chunk):
         near_copy(0, r).wait_send()
@@ -258,13 +274,18 @@
         full[core, chunk(r), :] = total.astype(BF16).astype(F32)
         back_copy(r).start()
 
-    sends = []
     gain_row2 = gain_m[...].astype(F32).reshape(1, dim)
     tile = 512
-    per_half = n_chunk // N_HALF
-    half_rows = n_seqs // N_HALF
-    for m in range(N_HALF):
-        chunks = range(m * per_half, (m + 1) * per_half)
+    outputs = [pltpu.make_async_copy(k_scr, knew_hbm, out_sem.at[2 * len(PARTS)]),
+               pltpu.make_async_copy(v_scr, vnew_hbm, out_sem.at[2 * len(PARTS) + 1])]
+    for c in outputs:
+        c.start()
+    for r in range(*PARTS[0]):
+        sum_far_y(r)
+    for m, (lo_chunk, hi_chunk) in enumerate(PARTS):
+        chunks = range(lo_chunk, hi_chunk)
+        n_rows = len(chunks) * ROWS
+
         def normalize(r):
             back_copy(r).wait_recv()
             x0 = full[0, chunk(r), :]
@@ -277,47 +298,48 @@
             h_scr[at, half_dim:] = (x1 * inv * gain_row2[:, half_dim:]).astype(BF16)
 
         for r in chunks:
-            sum_far_y(r)
-            if r > chunks[0]:
-                normalize(r - 1)
-        normalize(chunks[-1])
+            normalize(r)
         if m == 0:
             for c in w_copies[:2 * W_PARTS]:
                 c.wait()
 
-        def up_tile(n, carry):
+        def up_tile(n, carry, n_rows=n_rows):
             cols = pl.ds(pl.multiple_of(n * tile, tile), tile)
-            h2 = h_scr[0:half_rows, :]
+            h2 = h_scr[0:n_rows, :]
             gate = jnp.dot(h2, wg_v[:, cols], preferred_element_type=F32).astype(BF16).astype(F32)
             up = jnp.dot(h2, wu_v[:, cols], preferred_element_type=F32).astype(BF16).astype(F32)
-            a_scr[:, cols] = (gate * jax.nn.sigmoid(gate) * up).astype(BF16)
+            a_scr[0:n_rows, cols] = (gate * jax.nn.sigmoid(gate) * up).astype(BF16)
             return carry
 
         lax.fori_loop(0, ffn // tile, up_tile, 0)
         if m == 0:
             for c in w_copies[2 * W_PARTS:]:
                 c.wait()
-        half_at = pl.ds(m * half_rows, half_rows)
+        part_at = pl.ds(lo_chunk * ROWS, n_rows)
         for s in (other, core):
-            def down_tile(n, carry, s=s):
+            def down_tile(n, carry, s=s, part_at=part_at, n_rows=n_rows):
                 cols = pl.ds(pl.multiple_of(s * half_dim + n * tile, tile), tile)
-                part[s, half_at, pl.ds(pl.multiple_of(n * tile, tile), tile)] = jnp.dot(
-                    a_scr[...], wd_v[:, cols], preferred_element_type=F32)
+                part[s, part_at, pl.ds(pl.multiple_of(n * tile, tile), tile)] = jnp.dot(
+                    a_scr[0:n_rows, :], wd_v[:, cols], preferred_element_type=F32)
                 return carry
 
             lax.fori_loop(0, half_dim // tile, down_tile, 0)
             if s is other:
                 for r in chunks:
                     near_copy(1, r).start()
+        if m + 1 < len(PARTS):
+            for r in range(*PARTS[m + 1]):
+                sum_far_y(r)
         for r in chunks:
             near_copy(1, r).wait_recv()
             zsum[chunk(r), :] = part[core, chunk(r), :] + near[chunk(r), :]
-        sends += [pltpu.make_async_copy(full.at[core, half_at], x1_hbm.at[half_at], out_sem.at[4 + m]),
-                  pltpu.make_async_copy(zsum.at[half_at], send_hbm.at[half_at], out_sem.at[2 + m])]
-        for c in sends[-2:]:
+        sends = (pltpu.make_async_copy(full.at[core, part_at], x1_hbm.at[part_at], out_sem.at[2 * m]),
+                 pltpu.make_async_copy(zsum.at[part_at], send_hbm.at[part_at], out_sem.at[2 * m + 1]))
+        for c in sends:
             c.start()
-
-    for c in (*new_copies, *sends):
+        outputs += sends
+
+    for c in outputs:
         c.wait()
     for r in range(n_chunk):
         near_copy(1, r).wait_send()
@@ -346,21 +368,21 @@
             pltpu.VMEM((1, n_seqs), jnp.int32), pltpu.VMEM(freq.shape, F32), pltpu.VMEM((n_seqs, dim), BF16),
             pltpu.VMEM((dim,), BF16), pltpu.VMEM((dim,), BF16),
             pltpu.VMEM(w_query.shape, BF16), pltpu.VMEM(w_key.shape, BF16), pltpu.VMEM(w_value.shape, BF16),
-            pltpu.VMEM((2, ROWS * PAIR, cache_len), BF16), pltpu.VMEM((2, ROWS * PAIR, cache_len), BF16),
+            pltpu.VMEM((2, BLOCK * PAIR, cache_len), BF16), pltpu.VMEM((2, BLOCK * PAIR, cache_len), BF16),
             pltpu.VMEM((2, w_out.shape[0], half), BF16), pltpu.VMEM(w_gate.shape, BF16),
             pltpu.VMEM(w_up.shape, BF16), pltpu.VMEM(w_down.shape, BF16),
-            pltpu.VMEM((n_seqs, dim), BF16), pltpu.VMEM((n_seqs // N_HALF, ffn), BF16),
+            pltpu.VMEM((n_seqs, dim), BF16), pltpu.VMEM((max(hi - lo for lo, hi in PARTS) * ROWS, ffn), BF16),
             pltpu.VMEM((GROUP, n_seqs, PAIR), F32), pltpu.VMEM((n_seqs, PAIR), F32),
             pltpu.VMEM((n_seqs, PAIR), F32), pltpu.VMEM((n_seqs, PAIR), F32),
-            pltpu.VMEM((2 * GROUP * ROWS, cache_len), F32), pltpu.VMEM((2 * GROUP * ROWS, cache_len), BF16),
-            pltpu.VMEM((2 * GROUP * ROWS, PAIR), F32),
+            pltpu.VMEM((2 * GROUP * BLOCK, cache_len), F32), pltpu.VMEM((2 * GROUP * BLOCK, cache_len), BF16),
+            pltpu.VMEM((2 * GROUP * BLOCK, PAIR), F32),
             pltpu.VMEM((2, n_seqs, half), F32), pltpu.VMEM((n_seqs, half), F32),
             pltpu.VMEM((n_seqs, half), F32), pltpu.VMEM((n_seqs, half), F32),
             pltpu.VMEM((2, n_seqs, half), F32), pltpu.VMEM((n_seqs, half), F32),
             pltpu.SemaphoreType.DMA((8,)), pltpu.SemaphoreType.DMA((2, 2)), pltpu.SemaphoreType.DMA((16,)),
-            pltpu.SemaphoreType.DMA((3 * W_PARTS,)), pltpu.SemaphoreType.DMA((6,)),
+            pltpu.SemaphoreType.DMA((3 * W_PARTS,)), pltpu.SemaphoreType.DMA((2 + 2 * len(PARTS),)),
             sems, sems, sems, sems, sems, sems],
-        compiler_params=pltpu.CompilerParams(collective_id=0, has_side_effects=True, vmem_limit_bytes=67043328),
+        compiler_params=pltpu.CompilerParams(collective_id=0, has_side_effects=True, vmem_limit_bytes=LAYER_VMEM),
         name="layer",
     )(*args)
 
@@ -468,6 +490,23 @@
     )((lax.axis_index('tp') % 2).reshape(1), mine, other)
 
 
+def total_kernel(x1_ref, send_ref, far_ref, out_ref):
+    out_ref[...] = x1_ref[...] + (send_ref[...] + far_ref[...])
+
+
+def total_call(x1, send, far):
+    n_seqs, half = x1.shape
+    rows = 128
+    one = pl.BlockSpec((rows, half), lambda i: (i, 0))
+    return pl.pallas_call(
+        total_kernel,
+        out_shape=jax.ShapeDtypeStruct(x1.shape, F32),
+        grid=(n_seqs // rows,), in_specs=[one] * 3, out_specs=one,
+        compiler_params=pltpu.CompilerParams(dimension_semantics=("arbitrary",), vmem_limit_bytes=16 << 20),
+        name="total",
+    )(x1, send, far)
+
+
 FAR = [(0, 2), (1, 3), (2, 0), (3, 1)]
 NEAR = [(0, 1), (1, 0), (2, 3), (3, 2)]
 
@@ -484,7 +523,7 @@
         far = lax.ppermute(send, 'tp', FAR)
         k_full, v_full = write_call(positions, knew, vnew, kc, vc, 0, n_seqs // SEQS)
         far, k_full, v_full = lax.optimization_barrier((far, k_full, v_full))
-        total = x1 + (send + far)
+        total = total_call(x1, send, far)
         total_other = lax.ppermute(total, 'tp', NEAR)
         resid_out = join_call(total, total_other)
         return resid_out, back(k_full), back(v_full)

time: 79.8 us -> 76.9 us (0.964)
  Pallas kernels: 72.3 us -> 69.9 us
  starting transfers between devices: 1.65 us -> 0.08 us
  other arithmetic: 1.49 us -> 0 us
  waiting for transfers between devices: 2.56 us -> 3.9 us
  local copies, waits for them, and re-layouts: 0.97 us -> 2.2 us
    pallas_call x1, Pallas kernels: 25 us -> 23.4 us  [write_call(): pl.pallas_call(functools.partial(write_kernel, first_step, n_steps), out_...]
    add x1 -> x0, other arithmetic: 1.49 us -> none  [layer_local(): total = x1 + (send + far)]
    ppermute x1, starting transfers between devices: 1.51 us -> 0.04 us  [layer_local(): far = lax.ppermute(send, 'tp', FAR)]
    ppermute x1, waiting for transfers between devices: 0.01 us -> 1.26 us  [layer_local(): far = lax.ppermute(send, 'tp', FAR)]
    unnamed x6 -> x8, local copies, waits for them, and re-layouts: 0.97 us -> 2.2 us
    pallas_call x1, Pallas kernels: 46.3 us -> 45.3 us  [layer_call(): pl.pallas_call(layer_kernel, out_shape=(jax.ShapeDtypeStruct((n_seqs, hal...]
  transfers between devices with their start and end apart: 2 -> 2, of which waited for: 1 -> 2; matrix products, arithmetic and copies ran while one was open for 0% -> 0% of each run, Pallas kernels for 31% -> 30%
where the time goes in v3:
time: 76.9 us; the launch traced here: 76.8 us
  Pallas kernels  69.9 us (91%)
  waiting for transfers between devices  3.9 us (5%)
  local copies, waits for them, and re-layouts  2.2 us (3%)
    pallas_call x1, Pallas kernels, layer_call(): pl.pallas_call(layer_kernel, out_shape=(jax.ShapeDtypeStruct((n_seqs, hal...  45.3 us
    pallas_call x1, Pallas kernels, write_call(): pl.pallas_call(functools.partial(write_kernel, first_step, n_steps), out_...  23.4 us
    ppermute x1, waiting for transfers between devices, layer_local(): total_other = lax.ppermute(total, 'tp', NEAR)  2.64 us
    unnamed x8, local copies, waits for them, and re-layouts  2.2 us
  transfers between devices with their start and end apart: 2, of which 2 were waited for; matrix products, arithmetic and copies ran while one was open for 0% of the time, Pallas kernels for 30%

profile of v3, /device:TPU:0, one launch (start us, length us, event | category | flops | bytes accessed | tf_op | source)
XLA Modules:
  0.0 76.8 jit_solution(2489184994175292888)
XLA Ops:
  0.6 45.3 %layer.1 = (f32[256,1024]{1,0:T(8,128)}, f32[256,1024]{1,0:T(8,128)}, f32[256,128]{1,0:T(8,128)}, f32[256,128]{1,0:T(8,128)}) custom-call(s32[1,256]{1,0:T(1,128)} %bitcast.18, f32[2,128]{1,0:T(2,128)} %constant.19.clone.freq_hbm, bf16[256,2048]{1,0:T(8,128)(2,1)} %resid_hbm.1, bf16[2048]{0:T(1024)(128)(2,1)} %gain_a_hbm.1, bf16[2048]{0:T(1024)(128)(2,1)} %gain_m_hbm.1, ...), custom_call_target="tpu_custom_call" | custom-call | tf_op jit(solution)/shard_map/layer/pallas_call | solution.py:361
  45.9 0.0 collective-permute-start
  46.0 0.0 copy-start
  46.0 0.0 copy-start.1
  46.0 23.4 %write.1 = (bf16[32768,256]{1,0:T(8,128)(2,1)}, bf16[32768,256]{1,0:T(8,128)(2,1)}) custom-call(s32[256]{0:T(256)} %pos_smem.1, f32[256,128]{1,0:T(8,128)} %get-tuple-element.14.knew_hbm, f32[256,128]{1,0:T(8,128)} %get-tuple-element.15.vnew_hbm, bf16[32768,256]{1,0:T(8,128)(2,1)} %bitcast.15, bf16[32768,256]{1,0:T(8,128)(2,1)} %bitcast.17), custom_call_target="tpu_custom_call" | custom-call | flops 10000000000 | bytes 67108864 | tf_op jit(solution)/shard_map/write/pallas_call | solution.py:455
  69.4 1.3 %collective-permute-done.far_ref = f32[256,1024]{1,0:T(8,128)S(1)} collective-permute-done((f32[256,1024]{1,0:T(8,128)}, f32[256,1024]{1,0:T(8,128)S(1)}, u32[]{:S(2)}, u32[]{:S(2)}) %collective-permute-start) | collective-permute-done | bytes 1048608 | tf_op jit(solution)/shard_map/ppermute | solution.py:523
  70.7 0.0 copy-start.2
  70.7 1.0 %copy-done.2 = f32[256,1024]{1,0:T(8,128)} copy-done((f32[256,1024]{1,0:T(8,128)}, f32[256,1024]{1,0:T(8,128)S(1)}, u32[]{:S(2)}) %copy-start.2) | copy-done | bytes 1048600
  71.6 0.0 copy-done
  71.6 0.0 copy-done.1
  71.6 0.0 copy-start.3
  71.6 1.2 %copy-done.3 = f32[256,1024]{1,0:T(8,128)S(1)} copy-done((f32[256,1024]{1,0:T(8,128)S(1)}, f32[256,1024]{1,0:T(8,128)}, u32[]{:S(2)}) %copy-start.3) | copy-done | bytes 1048600
  72.9 0.2 total.1.mine_ref
  73.0 0.0 collective-permute-start.1
  73.1 2.6 %collective-permute-done.1.other_ref = f32[256,1024]{1,0:T(8,128)S(1)} collective-permute-done((f32[256,1024]{1,0:T(8,128)S(1)}, f32[256,1024]{1,0:T(8,128)S(1)}, u32[]{:S(2)}, u32[]{:S(2)}) %collective-permute-start.1) | collective-permute-done | bytes 1048608 | tf_op jit(solution)/shard_map/ppermute | solution.py:527
  75.7 1.0 %join.1 = bf16[256,2048]{1,0:T(8,128)(2,1)} custom-call(s32[1]{0:T(128)} %bitcast.core_smem, f32[256,1024]{1,0:T(8,128)S(1)} %total.1.mine_ref, f32[256,1024]{1,0:T(8,128)S(1)} %collective-permute-done.1.other_ref), custom_call_target="tpu_custom_call" | custom-call | tf_op jit(solution)/shard_map/join/pallas_call | solution.py:482
Async XLA Ops:
  45.9 24.7 %collective-permute-start = (f32[256,1024]{1,0:T(8,128)}, f32[256,1024]{1,0:T(8,128)S(1)}, u32[]{:S(2)}, u32[]{:S(2)}) collective-permute-start(f32[256,1024]{1,0:T(8,128)} %get-tuple-element.13.send_ref), channel_id=1, source_target_pairs={{0,2},{1,3},{2,0},{3,1},{4,6},{5,7},{6,4},{7,5},{8,10},{9,11},{10,... | collective-permute-start | bytes 3145736 | tf_op jit(solution)/shard_map/ppermute | solution.py:523
  46.0 25.7 %copy-start = (f32[256,1024]{1,0:T(8,128)S(1)}, f32[256,1024]{1,0:T(8,128)}, u32[]{:S(2)}) copy-start(f32[256,1024]{1,0:T(8,128)} %get-tuple-element.12.x1_ref) | copy-start | bytes 3145732
  46.0 25.7 %copy-start.1 = (f32[256,1024]{1,0:T(8,128)S(1)}, f32[256,1024]{1,0:T(8,128)}, u32[]{:S(2)}) copy-start(f32[256,1024]{1,0:T(8,128)} %get-tuple-element.13.send_ref) | copy-start | bytes 3145732
  70.7 1.0 %copy-start.2 = (f32[256,1024]{1,0:T(8,128)}, f32[256,1024]{1,0:T(8,128)S(1)}, u32[]{:S(2)}) copy-start(f32[256,1024]{1,0:T(8,128)S(1)} %collective-permute-done.far_ref) | copy-start | bytes 3145732
  71.6 1.2 %copy-start.3 = (f32[256,1024]{1,0:T(8,128)S(1)}, f32[256,1024]{1,0:T(8,128)}, u32[]{:S(2)}) copy-start(f32[256,1024]{1,0:T(8,128)} %copy-done.2) | copy-start | bytes 3145732
  73.0 2.7 %collective-permute-start.1 = (f32[256,1024]{1,0:T(8,128)S(1)}, f32[256,1024]{1,0:T(8,128)S(1)}, u32[]{:S(2)}, u32[]{:S(2)}) collective-permute-start(f32[256,1024]{1,0:T(8,128)S(1)} %total.1.mine_ref), channel_id=1, source_target_pairs={{0,1},{1,0},{2,3},{3,2},{4,5},{5,4},{6,7},{7,6},{8,9},{9,8},{10,11... | collective-permute-start | bytes 3145736 | tf_op jit(solution)/shard_map/ppermute | solution.py:527

commit v4 on v3

--- a/solution.py
+++ b/solution.py
@@ -25,9 +25,11 @@
 SUB = 8
 ROWS = 32
 BLOCK = 32
+Z_IN = 1
 FIRST = 64
 PARTS = ((0, 4), (4, 8))
 LAYER_VMEM = 67043328
+WRITE_VMEM = 56 << 20
 W_PARTS = 4
 SLOTS = 16
 AHEAD = 16
@@ -53,7 +55,7 @@
                  x1_hbm, send_hbm, knew_hbm, vnew_hbm,
                  pos_v, freq_v, resid_v, gain_a, gain_m, wq_v, wk_v, wv_v, k_buf, v_buf, wo_v, wg_v, wu_v, wd_v,
                  h_scr, a_scr, q_scr, k_scr, v_scr, pos_scr, s_scr, p_scr, n_scr,
-                 part, near, mine, far, full, zsum,
+                 part, near, mine, far, full, zsum, zfar,
                  in_sem, kv_sem, wo_sem, w_sem, out_sem,
                  near_send, near_recv, far_send, far_recv, back_send, back_recv):
     tp = lax.axis_index("tp")
@@ -68,6 +70,8 @@
     ffn = wg_v.shape[1]
     n_chunk = n_seqs // ROWS
     block = BLOCK * PAIR
+    tile = 512
+    n_tile = half_dim // tile
 
     inputs = [pltpu.make_async_copy(src, dst, in_sem.at[i]) for i, (src, dst) in enumerate((
         (resid_hbm, resid_v), (gain_a_hbm, gain_a), (wq_hbm, wq_v), (wk_hbm, wk_v), (wv_hbm, wv_v),
@@ -105,8 +109,12 @@
     def chunk(r):
         return pl.ds(pl.multiple_of(r * ROWS, ROWS), ROWS)
 
-    def near_copy(k, r):
-        return remote(part.at[other, chunk(r)], near.at[chunk(r)], (near_send, near_recv), k, r, sibling)
+    def near_copy(r):
+        return remote(part.at[other, chunk(r)], near.at[chunk(r)], (near_send, near_recv), 0, r, sibling)
+
+    def near_copy_z(m, at, n):
+        cols = pl.ds(n * tile, tile)
+        return remote(part.at[other, at, cols], near.at[at, cols], (near_send, near_recv), 1, m * n_tile + n, sibling)
 
     def far_copy(r):
         return remote(mine.at[chunk(r)], far.at[chunk(r)], (far_send, far_recv), 0, r, partner)
@@ -114,8 +122,11 @@
     def back_copy(r):
         return remote(full.at[core, chunk(r)], full.at[core, chunk(r)], (back_send, back_recv), 0, r, sibling)
 
+    def far_copy_z(r):
+        return remote(zsum.at[chunk(r)], zfar.at[chunk(r)], (far_send, far_recv), 1, r, partner)
+
     def sum_near(r):
-        near_copy(0, r).wait_recv()
+        near_copy(r).wait_recv()
         mine[chunk(r), :] = part[core, chunk(r), :] + near[chunk(r), :]
         far_copy(r).start()
 
@@ -172,8 +183,6 @@
     pos_col = jnp.sum(jnp.where(diag, pos_v[...].astype(F32), 0.0), axis=1, keepdims=True)
     pos_scr[...] = jnp.broadcast_to(pos_col, (n_seqs, PAIR))
     project(0, FIRST)
-    for c in wo_copies:
-        c.wait()
     pl.semaphore_wait(barrier, 2)
 
     lane_q = lax.broadcasted_iota(jnp.int32, (SUB, PAIR), 1)
@@ -251,8 +260,14 @@
             def _sum(r=r):
                 sum_near(r - 1)
 
+            if slot == 0:
+                @pl.when(r == 0)
+                def _w_out():
+                    for c in wo_copies:
+                        c.wait()
+
             part[other, chunk(r), :] = jnp.dot(o, wo_v[other], preferred_element_type=F32)
-            near_copy(0, r).start()
+            near_copy(r).start()
             part[core, chunk(r), :] = jnp.dot(o, wo_v[core], preferred_element_type=F32)
 
             if slot == 0:
@@ -266,7 +281,7 @@
     lax.fori_loop(0, n_chunk // 2, pair_step, 0)
     sum_near(n_chunk - 1)
     for r in range(n_chunk):
-        near_copy(0, r).wait_send()
+        near_copy(r).wait_send()
 
     def sum_far_y(r):
         far_copy(r).wait_recv()
@@ -275,7 +290,6 @@
         back_copy(r).start()
 
     gain_row2 = gain_m[...].astype(F32).reshape(1, dim)
-    tile = 512
     outputs = [pltpu.make_async_copy(k_scr, knew_hbm, out_sem.at[2 * len(PARTS)]),
                pltpu.make_async_copy(v_scr, vnew_hbm, out_sem.at[2 * len(PARTS) + 1])]
     for c in outputs:
@@ -317,34 +331,45 @@
                 c.wait()
         part_at = pl.ds(lo_chunk * ROWS, n_rows)
         for s in (other, core):
-            def down_tile(n, carry, s=s, part_at=part_at, n_rows=n_rows):
+            for n in range(n_tile):
                 cols = pl.ds(pl.multiple_of(s * half_dim + n * tile, tile), tile)
-                part[s, part_at, pl.ds(pl.multiple_of(n * tile, tile), tile)] = jnp.dot(
+                part[s, part_at, n * tile:(n + 1) * tile] = jnp.dot(
                     a_scr[0:n_rows, :], wd_v[:, cols], preferred_element_type=F32)
-                return carry
-
-            lax.fori_loop(0, half_dim // tile, down_tile, 0)
-            if s is other:
-                for r in chunks:
-                    near_copy(1, r).start()
+                if s is other:
+                    near_copy_z(m, part_at, n).start()
         if m + 1 < len(PARTS):
             for r in range(*PARTS[m + 1]):
                 sum_far_y(r)
-        for r in chunks:
-            near_copy(1, r).wait_recv()
-            zsum[chunk(r), :] = part[core, chunk(r), :] + near[chunk(r), :]
+        for n in range(n_tile):
+            cols = slice(n * tile, (n + 1) * tile)
+            near_copy_z(m, part_at, n).wait_recv()
+            zsum[part_at, cols] = part[core, part_at, cols] + near[part_at, cols]
+        if m == 0:
+            for r in range(Z_IN):
+                far_copy_z(r).start()
+            part_at = pl.ds(Z_IN * ROWS, n_rows - Z_IN * ROWS)
+        send_at = pl.ds(part_at.start - Z_IN * ROWS, part_at.size)
         sends = (pltpu.make_async_copy(full.at[core, part_at], x1_hbm.at[part_at], out_sem.at[2 * m]),
-                 pltpu.make_async_copy(zsum.at[part_at], send_hbm.at[part_at], out_sem.at[2 * m + 1]))
+                 pltpu.make_async_copy(zsum.at[part_at], send_hbm.at[send_at], out_sem.at[2 * m + 1]))
         for c in sends:
             c.start()
         outputs += sends
 
+    for r in range(Z_IN):
+        far_copy_z(r).wait_recv()
+        zfar[chunk(r), :] = full[core, chunk(r), :] + (zsum[chunk(r), :] + zfar[chunk(r), :])
+    outputs.append(pltpu.make_async_copy(zfar, x1_hbm.at[pl.ds(0, Z_IN * ROWS)], out_sem.at[2 * len(PARTS) + 2]))
+    outputs[-1].start()
     for c in outputs:
         c.wait()
+    for m, (lo_chunk, hi_chunk) in enumerate(PARTS):
+        for n in range(n_tile):
+            near_copy_z(m, pl.ds(lo_chunk * ROWS, (hi_chunk - lo_chunk) * ROWS), n).wait_send()
     for r in range(n_chunk):
-        near_copy(1, r).wait_send()
         back_copy(r).wait_send()
         far_copy(r).wait_send()
+    for r in range(Z_IN):
+        far_copy_z(r).wait_send()
 
 
 def layer_call(resid_in, positions, kc, vc, gain_attn, w_query, w_key, w_value, w_out, gain_mlp, w_gate, w_up, w_down):
@@ -360,7 +385,7 @@
             w_query, w_key, w_value, kc, vc, w_out, w_gate, w_up, w_down)
     return pl.pallas_call(
         layer_kernel,
-        out_shape=(jax.ShapeDtypeStruct((n_seqs, half), F32), jax.ShapeDtypeStruct((n_seqs, half), F32),
+        out_shape=(jax.ShapeDtypeStruct((n_seqs, half), F32), jax.ShapeDtypeStruct((n_seqs - Z_IN * ROWS, half), F32),
                    jax.ShapeDtypeStruct((n_seqs, PAIR), F32), jax.ShapeDtypeStruct((n_seqs, PAIR), F32)),
         in_specs=[hbm] * len(args),
         out_specs=(hbm,) * 4,
@@ -379,8 +404,9 @@
             pltpu.VMEM((2, n_seqs, half), F32), pltpu.VMEM((n_seqs, half), F32),
             pltpu.VMEM((n_seqs, half), F32), pltpu.VMEM((n_seqs, half), F32),
             pltpu.VMEM((2, n_seqs, half), F32), pltpu.VMEM((n_seqs, half), F32),
+            pltpu.VMEM((Z_IN * ROWS, half), F32),
             pltpu.SemaphoreType.DMA((8,)), pltpu.SemaphoreType.DMA((2, 2)), pltpu.SemaphoreType.DMA((16,)),
-            pltpu.SemaphoreType.DMA((3 * W_PARTS,)), pltpu.SemaphoreType.DMA((2 + 2 * len(PARTS),)),
+            pltpu.SemaphoreType.DMA((3 * W_PARTS,)), pltpu.SemaphoreType.DMA((3 + 2 * len(PARTS),)),
             sems, sems, sems, sems, sems, sems],
         compiler_params=pltpu.CompilerParams(collective_id=0, has_side_effects=True, vmem_limit_bytes=LAYER_VMEM),
         name="layer",
@@ -460,7 +486,7 @@
         scratch_shapes=[buf, buf, pltpu.VMEM(knew.shape, F32), pltpu.VMEM(vnew.shape, F32), pltpu.SemaphoreType.DMA((2,)),
                         pltpu.SemaphoreType.DMA((2, SLOTS)), pltpu.SemaphoreType.DMA((2, SLOTS))],
         input_output_aliases={5 + i: i for i in range(len(prev))},
-        compiler_params=pltpu.CompilerParams(vmem_limit_bytes=60 << 20),
+        compiler_params=pltpu.CompilerParams(vmem_limit_bytes=WRITE_VMEM),
         cost_estimate=pl.CostEstimate(flops=10 ** 10, bytes_accessed=4 * SEQS * PAIR * cache_len * 2 * n_steps,
                                       transcendentals=0),
         name="write",
@@ -490,23 +516,6 @@
     )((lax.axis_index('tp') % 2).reshape(1), mine, other)
 
 
-def total_kernel(x1_ref, send_ref, far_ref, out_ref):
-    out_ref[...] = x1_ref[...] + (send_ref[...] + far_ref[...])
-
-
-def total_call(x1, send, far):
-    n_seqs, half = x1.shape
-    rows = 128
-    one = pl.BlockSpec((rows, half), lambda i: (i, 0))
-    return pl.pallas_call(
-        total_kernel,
-        out_shape=jax.ShapeDtypeStruct(x1.shape, F32),
-        grid=(n_seqs // rows,), in_specs=[one] * 3, out_specs=one,
-        compiler_params=pltpu.CompilerParams(dimension_semantics=("arbitrary",), vmem_limit_bytes=16 << 20),
-        name="total",
-    )(x1, send, far)
-
-
 FAR = [(0, 2), (1, 3), (2, 0), (3, 1)]
 NEAR = [(0, 1), (1, 0), (2, 3), (3, 2)]
 
@@ -523,7 +532,7 @@
         far = lax.ppermute(send, 'tp', FAR)
         k_full, v_full = write_call(positions, knew, vnew, kc, vc, 0, n_seqs // SEQS)
         far, k_full, v_full = lax.optimization_barrier((far, k_full, v_full))
-        total = total_call(x1, send, far)
+        total = x1 + jnp.pad(send + far, ((Z_IN * ROWS, 0), (0, 0)))
         total_other = lax.ppermute(total, 'tp', NEAR)
         resid_out = join_call(total, total_other)
         return resid_out, back(k_full), back(v_full)

time: 76.9 us -> 72 us (0.936)
  local copies, waits for them, and re-layouts: 2.2 us -> 0.01 us
  Pallas kernels: 69.9 us -> 68.2 us
  waiting for transfers between devices: 3.9 us -> 2.64 us
    unnamed x8 -> x4, local copies, waits for them, and re-layouts: 2.2 us -> 0.01 us
    pallas_call x1, Pallas kernels: 45.3 us -> 43.7 us  [layer_call(): pl.pallas_call(layer_kernel, out_shape=(jax.ShapeDtypeStruct((n_seqs, hal...]
    ppermute x1, waiting for transfers between devices: 1.26 us -> 0.01 us  [layer_local(): far = lax.ppermute(send, 'tp', FAR)]
  transfers between devices with their start and end apart: 2 -> 2, of which waited for: 2 -> 1; matrix products, arithmetic and copies ran while one was open for 0% -> 0% of each run, Pallas kernels for 30% -> 33%
where the time goes in v4:
time: 72 us; the launch traced here: 71.9 us
  Pallas kernels  68.2 us (95%)
  waiting for transfers between devices  2.64 us (4%)
  between operations  0.73 us (1%)
    pallas_call x1, Pallas kernels, layer_call(): pl.pallas_call(layer_kernel, out_shape=(jax.ShapeDtypeStruct((n_seqs, hal...  43.7 us
    pallas_call x1, Pallas kernels, write_call(): pl.pallas_call(functools.partial(write_kernel, first_step, n_steps), out_...  23.4 us
    ppermute x1, waiting for transfers between devices, layer_local(): total_other = lax.ppermute(total, 'tp', NEAR)  2.64 us
  transfers between devices with their start and end apart: 2, of which 1 were waited for; matrix products, arithmetic and copies ran while one was open for 0% of the time, Pallas kernels for 33%

profile of v4, /device:TPU:0, one launch (start us, length us, event | category | flops | bytes accessed | tf_op | source)
XLA Modules:
  0.0 71.9 jit_solution(1729171995023713837)
XLA Ops:
  0.6 43.7 %layer.1 = (f32[256,1024]{1,0:T(8,128)}, f32[224,1024]{1,0:T(8,128)}, f32[256,128]{1,0:T(8,128)}, f32[256,128]{1,0:T(8,128)}) custom-call(s32[1,256]{1,0:T(1,128)} %bitcast.18, f32[2,128]{1,0:T(2,128)} %constant.22.clone.freq_hbm, bf16[256,2048]{1,0:T(8,128)(2,1)} %resid_hbm.1, bf16[2048]{0:T(1024)(128)(2,1)} %gain_a_hbm.1, bf16[2048]{0:T(1024)(128)(2,1)} %gain_m_hbm.1, ...), custom_call_target="tpu_custom_call" | custom-call | tf_op jit(solution)/shard_map/layer/pallas_call | solution.py:386
  44.4 0.0 collective-permute-start
  44.4 0.0 copy-start.1
  44.4 0.0 copy-start
  44.4 23.4 %write.1 = (bf16[32768,256]{1,0:T(8,128)(2,1)}, bf16[32768,256]{1,0:T(8,128)(2,1)}) custom-call(s32[256]{0:T(256)} %pos_smem.1, f32[256,128]{1,0:T(8,128)} %get-tuple-element.14.knew_hbm, f32[256,128]{1,0:T(8,128)} %get-tuple-element.15.vnew_hbm, bf16[32768,256]{1,0:T(8,128)(2,1)} %bitcast.15, bf16[32768,256]{1,0:T(8,128)(2,1)} %bitcast.17), custom_call_target="tpu_custom_call" | custom-call | flops 10000000000 | bytes 67108864 | tf_op jit(solution)/shard_map/write/pallas_call | solution.py:481
  67.8 0.0 collective-permute-done
  67.9 0.0 copy-done.1
  67.9 0.1 add.13
  68.0 0.0 copy-done
  68.0 0.1 pad_add_fusion.mine_ref
  68.2 0.0 collective-permute-start.1
  68.2 2.6 %collective-permute-done.1.other_ref = f32[256,1024]{1,0:T(8,128)S(1)} collective-permute-done((f32[256,1024]{1,0:T(8,128)S(1)}, f32[256,1024]{1,0:T(8,128)S(1)}, u32[]{:S(2)}, u32[]{:S(2)}) %collective-permute-start.1) | collective-permute-done | bytes 1048608 | tf_op jit(solution)/shard_map/ppermute | solution.py:536
  70.9 1.0 %join.1 = bf16[256,2048]{1,0:T(8,128)(2,1)} custom-call(s32[1]{0:T(128)} %bitcast.core_smem, f32[256,1024]{1,0:T(8,128)S(1)} %pad_add_fusion.mine_ref, f32[256,1024]{1,0:T(8,128)S(1)} %collective-permute-done.1.other_ref), custom_call_target="tpu_custom_call" | custom-call | tf_op jit(solution)/shard_map/join/pallas_call | solution.py:508
Async XLA Ops:
  44.4 23.5 %collective-permute-start = (f32[224,1024]{1,0:T(8,128)}, f32[224,1024]{1,0:T(8,128)S(1)}, u32[]{:S(2)}, u32[]{:S(2)}) collective-permute-start(f32[224,1024]{1,0:T(8,128)} %get-tuple-element.13), channel_id=1, source_target_pairs={{0,2},{1,3},{2,0},{3,1},{4,6},{5,7},{6,4},{7,5},{8,10},{9,11},{10,... | collective-permute-start | bytes 2752520 | tf_op jit(solution)/shard_map/ppermute | solution.py:532
  44.4 23.5 %copy-start.1 = (f32[224,1024]{1,0:T(8,128)S(1)}, f32[224,1024]{1,0:T(8,128)}, u32[]{:S(2)}) copy-start(f32[224,1024]{1,0:T(8,128)} %get-tuple-element.13) | copy-start | bytes 2752516
  44.4 23.6 %copy-start = (f32[256,1024]{1,0:T(8,128)S(1)}, f32[256,1024]{1,0:T(8,128)}, u32[]{:S(2)}) copy-start(f32[256,1024]{1,0:T(8,128)} %get-tuple-element.12) | copy-start | bytes 3145732
  68.2 2.7 %collective-permute-start.1 = (f32[256,1024]{1,0:T(8,128)S(1)}, f32[256,1024]{1,0:T(8,128)S(1)}, u32[]{:S(2)}, u32[]{:S(2)}) collective-permute-start(f32[256,1024]{1,0:T(8,128)S(1)} %pad_add_fusion.mine_ref), channel_id=1, source_target_pairs={{0,1},{1,0},{2,3},{3,2},{4,5},{5,4},{6,7},{7,6},{8,9},{9,8},{10,11... | collective-permute-start | bytes 3145736 | tf_op jit(solution)/shard_map/ppermute | solution.py:536

commit v5 on v4

--- a/solution.py
+++ b/solution.py
@@ -26,7 +26,7 @@
 ROWS = 32
 BLOCK = 32
 Z_IN = 1
-FIRST = 64
+FIRST = 128
 PARTS = ((0, 4), (4, 8))
 LAYER_VMEM = 67043328
 WRITE_VMEM = 56 << 20
@@ -313,6 +313,10 @@
 
         for r in chunks:
             normalize(r)
+        x1_rows = chunks[0] * ROWS + (Z_IN * ROWS if m == 0 else 0)
+        x1_at = pl.ds(x1_rows, chunks[-1] * ROWS + ROWS - x1_rows)
+        outputs.append(pltpu.make_async_copy(full.at[core, x1_at], x1_hbm.at[x1_at], out_sem.at[2 * m]))
+        outputs[-1].start()
         if m == 0:
             for c in w_copies[:2 * W_PARTS]:
                 c.wait()
@@ -349,8 +353,7 @@
                 far_copy_z(r).start()
             part_at = pl.ds(Z_IN * ROWS, n_rows - Z_IN * ROWS)
         send_at = pl.ds(part_at.start - Z_IN * ROWS, part_at.size)
-        sends = (pltpu.make_async_copy(full.at[core, part_at], x1_hbm.at[part_at], out_sem.at[2 * m]),
-                 pltpu.make_async_copy(zsum.at[part_at], send_hbm.at[send_at], out_sem.at[2 * m + 1]))
+        sends = (pltpu.make_async_copy(zsum.at[part_at], send_hbm.at[send_at], out_sem.at[2 * m + 1]),)
         for c in sends:
             c.start()
         outputs += sends

time: 72 us -> 71.7 us (level)
  no operation moved by 1% of the time
where the time goes in v5:
time: 71.7 us; the launch traced here: 71.5 us
  Pallas kernels  67.8 us (95%)
  waiting for transfers between devices  2.64 us (4%)
  between operations  0.73 us (1%)
    pallas_call x1, Pallas kernels, layer_call(): pl.pallas_call(layer_kernel, out_shape=(jax.ShapeDtypeStruct((n_seqs, hal...  43.3 us
    pallas_call x1, Pallas kernels, write_call(): pl.pallas_call(functools.partial(write_kernel, first_step, n_steps), out_...  23.4 us
    ppermute x1, waiting for transfers between devices, layer_local(): total_other = lax.ppermute(total, 'tp', NEAR)  2.64 us
  transfers between devices with their start and end apart: 2, of which 1 were waited for; matrix products, arithmetic and copies ran while one was open for 0% of the time, Pallas kernels for 33%

profile of v5, /device:TPU:0, one launch (start us, length us, event | category | flops | bytes accessed | tf_op | source)
XLA Modules:
  0.0 71.5 jit_solution(13734505717546113071)
XLA Ops:
  0.6 43.3 %layer.1 = (f32[256,1024]{1,0:T(8,128)}, f32[224,1024]{1,0:T(8,128)}, f32[256,128]{1,0:T(8,128)}, f32[256,128]{1,0:T(8,128)}) custom-call(s32[1,256]{1,0:T(1,128)} %bitcast.18, f32[2,128]{1,0:T(2,128)} %constant.22.clone.freq_hbm, bf16[256,2048]{1,0:T(8,128)(2,1)} %resid_hbm.1, bf16[2048]{0:T(1024)(128)(2,1)} %gain_a_hbm.1, bf16[2048]{0:T(1024)(128)(2,1)} %gain_m_hbm.1, ...), custom_call_target="tpu_custom_call" | custom-call | tf_op jit(solution)/shard_map/layer/pallas_call | solution.py:389
  44.0 0.0 collective-permute-start
  44.0 0.0 copy-start.1
  44.0 0.0 copy-start
  44.1 23.4 %write.1 = (bf16[32768,256]{1,0:T(8,128)(2,1)}, bf16[32768,256]{1,0:T(8,128)(2,1)}) custom-call(s32[256]{0:T(256)} %pos_smem.1, f32[256,128]{1,0:T(8,128)} %get-tuple-element.14.knew_hbm, f32[256,128]{1,0:T(8,128)} %get-tuple-element.15.vnew_hbm, bf16[32768,256]{1,0:T(8,128)(2,1)} %bitcast.15, bf16[32768,256]{1,0:T(8,128)(2,1)} %bitcast.17), custom_call_target="tpu_custom_call" | custom-call | flops 10000000000 | bytes 67108864 | tf_op jit(solution)/shard_map/write/pallas_call | solution.py:484
  67.5 0.0 collective-permute-done
  67.5 0.0 copy-done.1
  67.5 0.1 add.13
  67.6 0.0 copy-done
  67.7 0.1 pad_add_fusion.mine_ref
  67.8 0.0 collective-permute-start.1
  67.8 2.6 %collective-permute-done.1.other_ref = f32[256,1024]{1,0:T(8,128)S(1)} collective-permute-done((f32[256,1024]{1,0:T(8,128)S(1)}, f32[256,1024]{1,0:T(8,128)S(1)}, u32[]{:S(2)}, u32[]{:S(2)}) %collective-permute-start.1) | collective-permute-done | bytes 1048608 | tf_op jit(solution)/shard_map/ppermute | solution.py:539
  70.5 1.0 %join.1 = bf16[256,2048]{1,0:T(8,128)(2,1)} custom-call(s32[1]{0:T(128)} %bitcast.core_smem, f32[256,1024]{1,0:T(8,128)S(1)} %pad_add_fusion.mine_ref, f32[256,1024]{1,0:T(8,128)S(1)} %collective-permute-done.1.other_ref), custom_call_target="tpu_custom_call" | custom-call | tf_op jit(solution)/shard_map/join/pallas_call | solution.py:511
Async XLA Ops:
  44.0 23.5 %collective-permute-start = (f32[224,1024]{1,0:T(8,128)}, f32[224,1024]{1,0:T(8,128)S(1)}, u32[]{:S(2)}, u32[]{:S(2)}) collective-permute-start(f32[224,1024]{1,0:T(8,128)} %get-tuple-element.13), channel_id=1, source_target_pairs={{0,2},{1,3},{2,0},{3,1},{4,6},{5,7},{6,4},{7,5},{8,10},{9,11},{10,... | collective-permute-start | bytes 2752520 | tf_op jit(solution)/shard_map/ppermute | solution.py:535
  44.0 23.5 %copy-start.1 = (f32[224,1024]{1,0:T(8,128)S(1)}, f32[224,1024]{1,0:T(8,128)}, u32[]{:S(2)}) copy-start(f32[224,1024]{1,0:T(8,128)} %get-tuple-element.13) | copy-start | bytes 2752516
  44.0 23.6 %copy-start = (f32[256,1024]{1,0:T(8,128)S(1)}, f32[256,1024]{1,0:T(8,128)}, u32[]{:S(2)}) copy-start(f32[256,1024]{1,0:T(8,128)} %get-tuple-element.12) | copy-start | bytes 3145732
  67.8 2.7 %collective-permute-start.1 = (f32[256,1024]{1,0:T(8,128)S(1)}, f32[256,1024]{1,0:T(8,128)S(1)}, u32[]{:S(2)}, u32[]{:S(2)}) collective-permute-start(f32[256,1024]{1,0:T(8,128)S(1)} %pad_add_fusion.mine_ref), channel_id=1, source_target_pairs={{0,1},{1,0},{2,3},{3,2},{4,5},{5,4},{6,7},{7,6},{8,9},{9,8},{10,11... | collective-permute-start | bytes 3145736 | tf_op jit(solution)/shard_map/ppermute | solution.py:539
